TPU v7x, 32 devices: a whole 2x2x4 slice. The times are simulated.
32 devices in a mesh: row: 8 (over y, x, core), col: 4 (over z).
Axes of the slice: x: 2, y: 2, z: 4, core: 2. Of those that a mesh axis runs over, the one named last changes fastest.
Arguments:
- ancestor: float32 [9, 9, 512, 512], P(None, None, 'row', 'col'), may hold values from -1 to 4, as said below
- inverse_first: float32 [2, 2, 512, 512], P(None, None, 'row', 'col'), may hold values from -1 to 2, as said below
- panel_first: float32 [1536, 2, 512], P('row', None, 'col'), may hold values from -0.15625 to 0.15625
- structure_first: int32 [1536], replicated, may hold values from 0 to 4607, as said below
- inverse_second: float32 [1, 1, 512, 512], P(None, None, 'row', 'col'), may hold values from -1 to 2, as said below
- panel_second: float32 [1536, 1, 512], P('row', None, 'col'), may hold values from -0.15625 to 0.15625
- structure_second: int32 [1536], replicated, may hold values from 0 to 5631, as said below
Outputs:
- row_first: float32 [2, 11, 512, 512], P(None, None, 'row', 'col')
- row_second: float32 [1, 12, 512, 512], P(None, None, 'row', 'col')
Inputs may be any that keep to these rules, and one draw needn't show every extreme that they name: `ancestor`: symmetric and positive definite as a matrix. `inverse_first`: symmetric and positive definite as a matrix. `inverse_second`: symmetric and positive definite as a matrix. `structure_first`: entries are distinct; every aligned group of 16 ancestor rows holds at most 6 entries, and some group holds exactly 6. `structure_second`: entries are distinct; every aligned group of 16 ancestor rows holds at most 6 entries, and some group holds exactly 6.
All inputs are finite; a program needn't handle non-finite values.
Results may differ from a plain program's by a relative error of at most 0.000075.
Values sent between devices are 32-bit elements; how exact they have to be, the bound alone decides.
A program may use at most 128 MiB of HBM per device.

v0:
```python
import jax
import jax.numpy as jnp
from jax import lax
from jax.sharding import PartitionSpec as P

TILE = 512
GRAIN = 16
CAP = 6


def open_packed(packed, row_height, col_width):
    return packed.reshape(packed.shape[0], packed.shape[1], row_height, col_width)


def close_packed(tiles):
    depth = tiles.shape[2] * tiles.shape[3] // 128
    return tiles.reshape(tiles.shape[0], tiles.shape[1], depth, 128)


def product(left, right, left_dim=1):
    return lax.dot_general(
        left,
        right,
        (((left_dim,), (0,)), ((), ())),
        precision=lax.Precision.HIGH,
        preferred_element_type=jnp.float32,
    )


def entry_ranks(structure):
    group = structure // GRAIN
    order = jnp.arange(structure.shape[0], dtype=jnp.int32)
    same = (group[:, None] == group[None, :]) & (order[None, :] < order[:, None])
    return jnp.sum(same.astype(jnp.int32), axis=1)


def slots_within(structure, ranks, height):
    owner = structure % TILE // height
    group = structure // TILE * (height // GRAIN) + structure % height // GRAIN
    return owner, group * CAP + ranks


def one_hot(marks, count):
    return (jnp.arange(count, dtype=jnp.int32)[:, None] == marks[None, :]).astype(jnp.float32)


def local_rows(structure, marks, count, height):
    row = structure // TILE * height + structure % height
    match = jnp.arange(count, dtype=jnp.int32)[:, None] == marks[None, :]
    return jnp.max(jnp.where(match, row[None, :], -1), axis=1)


def on_device(
    ancestor,
    inverse_first,
    panel_first,
    structure_first,
    inverse_second,
    panel_second,
    structure_second,
):
    rows = lax.axis_size("row")
    cols = lax.axis_size("col")
    height = TILE // rows
    width = TILE // cols
    halves = width // height
    row_index = lax.axis_index("row")
    col_index = lax.axis_index("col")
    blocks = open_packed(ancestor, height, width)
    first_diag = open_packed(inverse_first, height, width)
    second_diag = open_packed(inverse_second, height, width)
    tiles = blocks.shape[0]
    first = first_diag.shape[0]
    second = second_diag.shape[0]
    every = first + second
    limit = tiles * TILE
    first_width = first * width

    panels = jnp.concatenate(
        [panel_first.reshape(-1, first_width), panel_second.reshape(-1, second * width)], axis=1
    )
    both = lax.all_gather(panels, "row", axis=0, tiled=True)
    whole_first = both[:, :first_width]
    whole_second = both[:, first_width:]

    above = structure_second < limit
    ranks_first = entry_ranks(structure_first)
    ranks_second = entry_ranks(structure_second)
    row_slots = tiles * height // GRAIN * CAP
    col_slots = tiles * width // GRAIN * CAP
    low_slots = first * TILE // GRAIN * CAP
    owner, slot = slots_within(structure_first, ranks_first, height)
    row_marks_first = jnp.where(owner == row_index, slot, -1)
    owner, slot = slots_within(structure_second, ranks_second, height)
    row_marks_second = jnp.where(above & (owner == row_index), slot, -1)
    owner, slot = slots_within(structure_first, ranks_first, width)
    all_marks_first = owner * col_slots + slot
    col_marks_first = jnp.where(owner == col_index, slot, -1)
    owner, slot = slots_within(structure_second, ranks_second, width)
    all_marks_second = jnp.where(above, owner * col_slots + slot, -1)
    col_marks_second = jnp.where(above & (owner == col_index), slot, -1)
    below = structure_second - limit
    low_marks = jnp.where(above, -1, below // GRAIN * CAP + ranks_second)
    low_match = jnp.arange(low_slots, dtype=jnp.int32)[:, None] == low_marks[None, :]
    low_rows = jnp.max(jnp.where(low_match, below[None, :], -1), axis=1)

    take_first = one_hot(row_marks_first, row_slots)
    take_second = one_hot(
        jnp.where(above, row_marks_second, row_slots + low_marks), row_slots + low_slots
    )
    part_first = product(take_first, whole_first)
    part_second = product(take_second, whole_second)
    part_first = part_first.reshape(row_slots, first, halves, height).transpose(0, 2, 1, 3)
    part_first = part_first.reshape(row_slots * first, width)
    part_second = part_second.reshape(row_slots + low_slots, second, halves, height)
    part_second = part_second.transpose(0, 2, 1, 3)
    part_second = part_second.reshape((row_slots + low_slots) * second, width)
    spread = lax.all_gather(jnp.concatenate([part_first, part_second], axis=0), "col", axis=0)
    cut = part_first.shape[0]
    got_first = spread[:, :cut].reshape(cols, row_slots, halves, first, height)
    got_second = spread[:, cut:].reshape(cols, row_slots + low_slots, halves, second, height)
    got_first = got_first.transpose(1, 0, 2, 3, 4).reshape(row_slots, rows, first * height)
    got_second = got_second.transpose(1, 0, 2, 3, 4).reshape(-1, rows, second * height)
    upper_second = got_second[:row_slots]
    low_second = got_second[row_slots:].reshape(low_slots, second * TILE)

    flat = blocks.transpose(0, 2, 1, 3).reshape(tiles * height, tiles * width)
    kept_rows = jnp.concatenate(
        [
            local_rows(structure_first, row_marks_first, row_slots, height),
            local_rows(structure_second, row_marks_second, row_slots, height),
        ]
    )
    take_kept = (
        kept_rows[:, None] == jnp.arange(tiles * height, dtype=jnp.int32)[None, :]
    ).astype(jnp.float32)
    kept = product(take_kept, flat)

    place = jnp.arange(first * TILE, dtype=jnp.int32)
    place_row = place // (first * height)
    place_tile = place // height % first
    named = place_tile * TILE + place_row * height + place % height
    meet_low = (named[:, None] == low_rows[None, :]).astype(jnp.float32)
    first_at_low = product(got_first.reshape(row_slots, first * TILE), meet_low)
    folded = product(first_at_low, low_second).reshape(row_slots, rows, second * height)
    left = jnp.concatenate(
        [
            jnp.concatenate([got_first, -folded], axis=2),
            jnp.concatenate(
                [jnp.zeros((row_slots, rows, first * height), jnp.float32), upper_second], axis=2
            ),
        ],
        axis=0,
    )
    partial = product(left.reshape(2 * row_slots, every * TILE), kept, 0)
    partial = partial.reshape(rows, every * height, tiles * width)

    own_low = jnp.arange(first * height, dtype=jnp.int32)
    own_low = own_low // height * TILE + row_index * height + own_low % height
    own_meet = (own_low[:, None] == low_rows[None, :]).astype(jnp.float32)
    own_second = product(own_meet, low_second)
    flat_diag = first_diag.transpose(0, 2, 1, 3).reshape(first * height, first_width)
    low_partial = product(own_second, flat_diag, 0)
    low_partial = low_partial.reshape(rows, second * height, first_width)

    slabs = [low_partial[:, :, k * width : (k + 1) * width] for k in range(first)]
    slabs.append(jnp.zeros((rows, (every - first * second) * height, width), jnp.float32))
    joined = jnp.concatenate([partial, jnp.concatenate(slabs, axis=1)], axis=2)
    summed = lax.psum_scatter(joined, "row", scatter_dimension=0, tiled=False)
    image = summed[:, : tiles * width]
    step = second * height
    low_image = jnp.concatenate(
        [summed[k * step : (k + 1) * step, tiles * width :] for k in range(first)], axis=1
    )

    edge = first * height
    column_ids = jnp.arange(tiles * width, dtype=jnp.int32)
    col_rows_first = local_rows(structure_first, col_marks_first, col_slots, width)
    col_rows_second = local_rows(structure_second, col_marks_second, col_slots, width)
    pick_first = (column_ids[:, None] == col_rows_first[None, :]).astype(jnp.float32)
    pick_second = (column_ids[:, None] == col_rows_second[None, :]).astype(jnp.float32)
    picked = jnp.concatenate([product(image, pick_first), product(image[edge:], pick_second)], axis=0)
    met = lax.all_gather(picked, "col", axis=0)
    met = met.transpose(1, 0, 2).reshape(-1, cols * col_slots)
    dense_first = product(one_hot(all_marks_first, cols * col_slots), whole_first)
    dense_second = product(one_hot(all_marks_second, cols * col_slots), whole_second)
    corner = product(met[: every * height], dense_first)
    low_block = low_image - corner[edge:]
    low_all = lax.all_gather(low_block, "col", axis=0)
    low_all = low_all.transpose(1, 0, 2).reshape(second * height, first * TILE)
    spot = jnp.arange(first * TILE, dtype=jnp.int32)
    spot = spot // width % first * TILE + spot // first_width * width + spot % width
    below_marks = jnp.where(above, -1, below)
    dense_low = product(
        (spot[:, None] == below_marks[None, :]).astype(jnp.float32), whole_second
    )
    final = product(met[every * height :], dense_second) + product(low_all, dense_low)

    def tiled(matrix, up, across):
        return matrix.reshape(up, height, across, width).transpose(0, 2, 1, 3)

    row_first = jnp.concatenate(
        [-tiled(image[:edge], first, tiles), first_diag + tiled(corner[:edge], first, first)], axis=1
    )
    row_second = jnp.concatenate(
        [
            -tiled(image[edge:], second, tiles),
            -tiled(low_block, second, first),
            second_diag + tiled(final, second, second),
        ],
        axis=1,
    )
    return (close_packed(row_first), close_packed(row_second))


def solution(mesh):
    in_specs = (
        P(None, None, "row", "col"),
        P(None, None, "row", "col"),
        P("row", None, "col"),
        P(),
        P(None, None, "row", "col"),
        P("row", None, "col"),
        P(),
    )
    out_specs = (P(None, None, "row", "col"), P(None, None, "row", "col"))
    return jax.shard_map(
        on_device, mesh=mesh, in_specs=in_specs, out_specs=out_specs, check_vma=False
    )
```

profile of v0, /device:TPU:0, one launch (start us, length us, event | category | flops | bytes accessed | tf_op | source)
XLA Modules:
  0.0 274.7 jit_solution(11923540824336374075)
XLA Ops:
  11.3 2.7 convert_reduce_fusion
  14.7 2.7 convert_reduce_fusion.1
  18.1 23.9 %all-gather.7.cloned.1.call-done = f32[1536,384]{1,0:T(8,128)} async-done(((f32[192,384]{1,0:T(8,128)}), f32[1536,384]{1,0:T(8,128)}) %all-gather.7.cloned.1.call-update) | async-done | bytes 2359312 | tf_op jit(solution)/shard_map/all_gather | solution.py:82
  42.1 2.4 fusion.28
  45.1 2.4 fusion.8
  52.7 2.4 convolution_bitcast_fusion
  55.1 39.3 %all-gather.9.cloned.1.call-done = f32[4128,128]{1,0:T(8,128)} async-done(((f32[1032,128]{1,0:T(8,128)}), f32[4128,128]{1,0:T(8,128)}) %all-gather.9.cloned.1.call-update) | async-done | bytes 2113552 | tf_op jit(solution)/shard_map/all_gather | solution.py:118
  94.4 2.4 slice.87
  96.8 1.7 copy.42
  102.4 2.2 reshape.189
  104.7 3.1 %copy.30 = f32[216,4,2,2,64]{0,4,3,2,1:T(8,128)S(1)} copy(f32[216,4,2,2,64]{4,3,2,0,1:T(2,128)} %bitcast.81) | data formatting | bytes 1769472 | tf_op jit(solution)/shard_map/transpose | solution.py:122
  108.8 1.7 convolution_negate_fusion
  110.6 6.3 %fusion.10 = f32[8,192,1152]{2,1,0:T(8,128)S(1)} fusion(f32[432,1152,1]{1,0,2:T(8,128)S(1)} %convolution_bitcast_fusion, f32[216,8,64]{0,2,1:T(8,128)S(1)} %bitcast.88, f32[216,8,64]{0,2,1:T(8,128)S(1)} %convolution_negate_fusion, f32[216,8,128]{0,2,1:T(8,128)S(1)} %bitcast.76), kind=kOutput, calls=%fused_computation.18 | convolution fusion | flops 4589125632 | bytes 10838016 | tf_op jit(solution)/shard_map/dot_general | solution.py:21
  116.9 3.9 %maximum_maximum_fusion = f32[8,192,1280]{2,1,0:T(8,128)} fusion(f32[8,64,128]{2,1,0:T(8,128)S(1)} %copy-done.6, f32[8,64,128]{2,1,0:T(8,128)S(1)} %get-tuple-element.18, f32[8,192,1152]{2,1,0:T(8,128)S(1)} %fusion.10, f32[192,1280]{1,0:T(8,128)S(1)} %copy-done.2), kind=kLoop, calls=%fused_computation.9 | loop fusion | flops 5898240 | bytes 16449536 | tf_op jit(solution)/shard_map/concatenate | solution.py:168
  121.9 67.3 %reduce-scatter.2.cloned.1.call-done = f32[1,192,1280]{2,1,0:T(8,128)} async-done(((f32[8,192,1280]{2,1,0:T(8,128)}), f32[1,192,1280]{2,1,0:T(8,128)}) %reduce-scatter.2.cloned.1.call-update) | async-done | bytes 983056 | tf_op jit(solution)/shard_map/reduce_scatter | solution.py:169
  189.2 1.7 fusion.21
  190.9 2.0 fusion.20
  193.8 2.6 fusion.4
  196.5 3.9 %fusion.1 = f32[1728,128]{1,0:T(8,128)} fusion(s32[1536]{0:T(1024)S(1)} %get-tuple-element.8, f32[1536,384]{1,0:T(8,128)S(1)} %copy-done.7), kind=kOutput, calls=%fused_computation.3 | convolution fusion | flops 2041085952 | bytes 1679360 | tf_op jit(solution)/shard_map/dot_general | solution.py:21
  200.3 4.3 %fusion = f32[1728,256]{1,0:T(8,128)} fusion(s32[1536]{0:T(1024)S(1)} %get-tuple-element.11, f32[1536,384]{1,0:T(8,128)S(1)} %copy-done.7), kind=kOutput, calls=%fused_computation.2 | convolution fusion | flops 4079517696 | bytes 3350528 | tf_op jit(solution)/shard_map/dot_general | solution.py:21
  206.6 33.0 %all-gather.11.cloned.1.call-done = f32[1024,432]{1,0:T(8,128)} async-done(((f32[256,432]{1,0:T(8,128)}), f32[1024,432]{1,0:T(8,128)}) %all-gather.11.cloned.1.call-update) | async-done | bytes 1769488 | tf_op jit(solution)/shard_map/all_gather | solution.py:183
  239.6 3.1 %copy.53 = f32[4,256,432]{2,0,1:T(4,128)S(1)} copy(f32[4,256,432]{2,1,0:T(8,128)} %bitcast.89) | data formatting | bytes 3538944 | tf_op jit(solution)/shard_map/all_gather | solution.py:183
  245.3 2.3 fusion.134
  250.4 14.1 %all-gather.2 = f32[256,256]{1,0:T(8,128)S(1)} all-gather(f32[64,256]{1,0:T(8,128)S(1)} %get-tuple-element.7), channel_id=4, replica_groups=mesh['row'=8,'col'=4] {'col'}, dimensions={0}, use_global_device_ids=true | all-gather | bytes 327680 | tf_op jit(solution)/shard_map/all_gather | solution.py:189
  (92 shorter events, 28.7 us)
Async XLA Ops:
  7.2 34.9 %all-gather.7.cloned.1.call-start = ((), (), s32[]{:S(2)}) async-start(), calls=%async_computation.1 | async-start | bytes 2654208 | tf_op jit(solution)/shard_map/all_gather | solution.py:82
  9.8 84.6 %all-gather.9.cloned.1.call-start = ((), (), s32[]{:S(2)}) async-start(), calls=%async_computation.3 | async-start | bytes 2641920 | tf_op jit(solution)/shard_map/all_gather | solution.py:118
  44.5 4.2 %copy-start.11 = (f32[2,2,64,128]{3,2,1,0:T(8,128)S(1)}, f32[2,2,64,128]{3,2,1,0:T(8,128)}, u32[]{:S(2)}) copy-start(f32[2,2,64,128]{3,2,1,0:T(8,128)} %param.8) | copy-start | bytes 393220
  44.8 4.1 %copy-start.3 = (f32[9,9,64,128]{3,2,1,0:T(8,128)S(1)}, f32[9,9,64,128]{3,2,1,0:T(8,128)}, u32[]{:S(2)}) copy-start(f32[9,9,64,128]{3,2,1,0:T(8,128)} %param.7) | copy-start | bytes 7962628
  48.3 140.9 %reduce-scatter.2.cloned.1.call-start = ((), (), s32[]{:S(2)}) async-start(), calls=%async_computation.2 | async-start | bytes 8847360 | tf_op jit(solution)/shard_map/reduce_scatter | solution.py:169
  48.9 2.8 %copy-start.13 = (s32[1536]{0:T(1024)S(1)}, s32[1536]{0:T(1024)}, u32[]{:S(2)}) copy-start(s32[1536]{0:T(1024)} %param.10) | copy-start | bytes 18436
  98.7 2.9 %copy-start = (f32[384,4,2,1,64]{0,4,2,1,3:T(8,128)}, f32[384,4,2,1,64]{0,4,2,1,3:T(8,128)S(1)}, u32[]{:S(2)}) copy-start(f32[384,4,2,1,64]{0,4,2,1,3:T(8,128)S(1)} %slice.88) | copy-start | bytes 2359300
  107.8 2.7 copy-start.4
  110.6 6.3 %copy-start.2 = (f32[192,1280]{1,0:T(8,128)S(1)}, f32[192,1280]{1,0:T(8,128)}, u32[]{:S(2)}) copy-start(f32[192,1280]{1,0:T(8,128)} %pad.13.clone) | copy-start | bytes 2949124
  110.6 6.3 %copy-start.6 = (f32[8,64,128]{2,1,0:T(8,128)S(1)}, f32[8,64,128]{2,1,0:T(8,128)}, u32[]{:S(2)}) copy-start(f32[8,64,128]{2,1,0:T(8,128)} %get-tuple-element.19) | copy-start | bytes 786436
  120.8 73.0 %copy-start.7 = (f32[1536,384]{1,0:T(8,128)S(1)}, f32[1536,384]{1,0:T(8,128)}, u32[]{:S(2)}) copy-start(f32[1536,384]{1,0:T(8,128)} %all-gather.7.cloned.1.call-done) | copy-start | bytes 7077892
  120.8 118.8 %all-gather.11.cloned.1.call-start = ((), (), s32[]{:S(2)}) async-start(), calls=%async_computation.4 | async-start | bytes 2621440 | tf_op jit(solution)/shard_map/all_gather | solution.py:183
  200.3 4.3 %copy-start.8 = (f32[1,192,1280]{2,1,0:T(8,128)S(1)}, f32[1,192,1280]{2,1,0:T(8,128)}, u32[]{:S(2)}) copy-start(f32[1,192,1280]{2,1,0:T(8,128)} %reduce-scatter.2.cloned.1.call-done) | copy-start | bytes 2949124
  245.2 2.5 copy-start.12
  245.2 3.0 %copy-start.1 = (f32[2,64,9,128]{3,2,1,0:T(8,128)S(1)}, f32[2,64,9,128]{3,2,1,0:T(8,128)}, u32[]{:S(2)}) copy-start(f32[2,64,9,128]{3,2,1,0:T(8,128)} %neg.32) | copy-start | bytes 1769476
  247.6 0.7 copy-start.10
  248.3 16.4 %copy-start.5 = (f32[64,4,432]{2,1,0:T(4,128)S(1)}, f32[64,4,432]{2,1,0:T(4,128)}, u32[]{:S(2)}) copy-start(f32[64,4,432]{2,1,0:T(4,128)} %slice.100) | copy-start | bytes 1327108
  248.4 18.1 %copy-start.9 = (f32[1728,128]{1,0:T(8,128)S(1)}, f32[1728,128]{1,0:T(8,128)}, u32[]{:S(2)}) copy-start(f32[1728,128]{1,0:T(8,128)} %fusion.1) | copy-start | bytes 2654212
  248.4 18.1 %copy-start.14 = (f32[1,1,64,128]{3,2,1,0:T(8,128)S(1)}, f32[1,1,64,128]{3,2,1,0:T(8,128)}, u32[]{:S(2)}) copy-start(f32[1,1,64,128]{3,2,1,0:T(8,128)} %param.11) | copy-start | bytes 98308
Sparse Core Ops, SparseCore 0:
  10.4 31.5 all-gather.6
  48.4 45.9 all-gather.8
  121.0 68.2 reduce-scatter.1
  193.9 45.6 all-gather.10
where the time goes:
time: 280 us; the launch traced here: 275 us
  waiting for transfers between devices  164 us (59%)
  matrix products  35.5 us (13%)
  local copies, waits for them, and re-layouts  27.7 us (10%)
  other arithmetic  18.6 us (7%)
  between operations  14.5 us (5%)
  blocking collectives  14.1 us (5%)
    reduce_scatter x1, waiting for transfers between devices, on_device(): summed = lax.psum_scatter(joined, 'row', scatter_dimension=0, tiled=False)  67.3 us
    all_gather x1, waiting for transfers between devices, on_device(): lax.all_gather(jnp.concatenate([part_first, part_second], axis=0), 'col',...  39.3 us
    dot_general x16, matrix products, product(): lax.dot_general(left, right, (((left_dim,), (0,)), ((), ())), precision=l...  35.5 us
    all_gather x1, waiting for transfers between devices, on_device(): met = lax.all_gather(picked, 'col', axis=0)  33 us
    all_gather x1, waiting for transfers between devices, on_device(): both = lax.all_gather(panels, 'row', axis=0, tiled=True)  23.9 us
    all_gather x1, blocking collectives, on_device(): low_all = lax.all_gather(low_block, 'col', axis=0)  14.1 us
  transfers between devices with their start and end apart: 4, of which 4 were waited for; matrix products, arithmetic and copies ran while one was open for 10% of the time, Pallas kernels for 0%

commit v1 on v0

--- a/solution.py
+++ b/solution.py
@@ -1,6 +1,10 @@
+import functools
+
 import jax
 import jax.numpy as jnp
 from jax import lax
+from jax.experimental import pallas as pl
+from jax.experimental.pallas import tpu as pltpu
 from jax.sharding import PartitionSpec as P
 
 TILE = 512
@@ -212,8 +216,618 @@
     )
     return (close_packed(row_first), close_packed(row_second))
 
+F32 = jnp.float32
+BF16 = jnp.bfloat16
+MESH = pl.DeviceIdType.MESH
+
+
+def over(value, size):
+    return lax.shift_right_logical(value, jnp.int32(size.bit_length() - 1))
+
+
+def within(value, size):
+    return value & jnp.int32(size - 1)
+
+
+def iota(shape, dim):
+    return lax.broadcasted_iota(jnp.int32, shape, dim)
+
+
+def ones_at(mask):
+    return jnp.where(mask, 1.0, 0.0).astype(BF16)
+
+
+def dd(left, right, left_dim=1, right_dim=0):
+    return lax.dot_general(
+        left, right, (((left_dim,), (right_dim,)), ((), ())), preferred_element_type=F32
+    )
+
+
+def halves_of(value):
+    high = value.astype(BF16)
+    return high, (value - high.astype(F32)).astype(BF16)
+
+
+def three(left, right):
+    return dd(left[0], right[0]) + dd(left[0], right[1]) + dd(left[1], right[0])
+
+
+def grown(value, count):
+    rest = count - value.shape[0]
+    return jnp.concatenate([value, jnp.zeros((rest, value.shape[1]), value.dtype)], axis=0)
+
+
+def spots(hits, places):
+    return jnp.max(jnp.where(hits, places, -1.0), axis=1, keepdims=True)
+
+
+def fused(dims, names, *refs):
+    ref = dict(zip(names, refs))
+    rows, cols, height, width, tiles, first, entries = dims
+    chunks = first + 1
+    shard = entries // rows
+    wide = tiles * width
+    tall = tiles * height
+    row_slots = tall // GRAIN * CAP
+    low_slots = first * height // GRAIN * CAP
+    col_slots = wide // GRAIN * CAP
+    edge = first * height
+    row_pad = -(-row_slots // 128) * 128
+    col_pad = -(-col_slots // 128) * 128
+    half = height // 2
+
+    r = lax.axis_index("row")
+    c = lax.axis_index("col")
+    core = r % 2
+    chip = r // 2
+    chip_x = chip % 2
+    chip_y = chip // 2
+    by_x = r + 2 - 4 * chip_x
+    by_y = r + 4 - 8 * chip_y
+    by_both = r + 6 - 4 * chip_x - 8 * chip_y
+    mate = r + 1 - 2 * core
+    peers = {1: by_x, 2: by_y, 3: by_both}
+
+    def chip_at(rel):
+        x = 1 - chip_x if rel % 2 else chip_x
+        y = 1 - chip_y if rel // 2 else chip_y
+        return y * 2 + x
+
+    sent = []
+
+    def remote(source, target, send, recv, device, column=None):
+        return pltpu.make_async_remote_copy(
+            src_ref=source,
+            dst_ref=target,
+            send_sem=send,
+            recv_sem=recv,
+            device_id=(device, c if column is None else column),
+            device_id_type=MESH,
+        )
+
+    def launch(copy):
+        copy.start()
+        sent.append((None, copy))
+        return copy
+
+    barrier = pltpu.get_barrier_semaphore()
+    for peer in (mate, by_x, by_y, by_both):
+        pl.semaphore_signal(barrier, inc=1, device_id=(peer, c), device_id_type=MESH)
+    for step in range(1, cols):
+        other = (c + step) % cols
+        pl.semaphore_signal(barrier, inc=1, device_id=(r, other), device_id_type=MESH)
+    pl.semaphore_wait(barrier, 4 + cols - 1)
+
+    panel = ref["panel"]
+    pall = ref["pall"]
+
+    def own_rows(device):
+        return pl.ds(pl.multiple_of(device * shard, 8), shard)
+
+    gather = {}
+    for k in range(chunks):
+        for rel, peer in peers.items():
+            gather[k, rel] = launch(
+                remote(
+                    panel.at[k],
+                    pall.at[k, own_rows(r)],
+                    ref["g_send"].at[k, rel],
+                    ref["g_recv"].at[k, rel],
+                    peer,
+                )
+            )
+        gather[k, 0] = launch(
+            remote(
+                panel.at[k],
+                pall.at[k, own_rows(r)],
+                ref["g_send"].at[k, 0],
+                ref["g_recv"].at[k, 0],
+                mate,
+            )
+        )
+    for k in range(chunks):
+        pall[k, own_rows(r), :] = panel[k]
+
+    def ranks(row, which):
+        group = over(row, GRAIN)
+        at = iota((1, entries), 1)
+
+        def step(b, total):
+            start = pl.multiple_of(b * 128, 128)
+            column = over(ref["scol"][pl.ds(start, 128), which : which + 1], GRAIN)
+            order = iota((128, 1), 0) + b * 128
+            hit = (column == group) & (order < at)
+            return total + jnp.sum(jnp.where(hit, 1.0, 0.0), axis=0, keepdims=True)
+
+        total = lax.fori_loop(0, entries // 128, step, jnp.zeros((1, entries), F32))
+        return total.astype(jnp.int32)
+
+    def owned(row, rank, size):
+        owner = over(within(row, TILE), size)
+        group = over(row, TILE) * (size // GRAIN) + over(within(row, size), GRAIN)
+        place = over(row, TILE) * size + within(row, size)
+        return owner, group * CAP + rank, place.astype(F32)
+
+    row1 = ref["srow"][0:1, :]
+    row2 = ref["srow"][1:2, :]
+    rank1 = ranks(row1, 0)
+    rank2 = ranks(row2, 1)
+    above = row2 < tiles * TILE
+    r_owner1, r_slot1, r_place1 = owned(row1, rank1, height)
+    r_owner2, r_slot2, r_place2 = owned(row2, rank2, height)
+    c_owner1, c_slot1, c_place1 = owned(row1, rank1, width)
+    c_owner2, c_slot2, c_place2 = owned(row2, rank2, width)
+    mark1 = jnp.where(r_owner1 == r, r_slot1, -1)
+    mark2 = jnp.where(r_owner2 == r, r_slot2, -1)
+    upper2 = jnp.where(above, mark2, -1)
+    lower2 = jnp.where(above | (r_owner2 != r), -1, r_slot2 - row_slots)
+
+    def keep(at, marks, places):
+        spot = spots(iota((row_pad, entries), 0) == marks, places)
+        take = ones_at(spot == iota((row_pad, tall), 1).astype(F32))
+
+        def step(j, carry):
+            block = ref["ancestor"][:, pl.ds(j, 1), :, :].reshape(tall, width)
+            high, low = halves_of(block)
+            span = pl.ds(pl.multiple_of(j * width, 128), width)
+            ref["kept_h"][at, :, span] = dd(take, high).astype(BF16)
+            ref["kept_l"][at, :, span] = dd(take, low).astype(BF16)
+            return carry
+
+        lax.fori_loop(0, tiles, step, 0)
+
+    keep(0, mark1, r_place1)
+
+    def z_step(d, at, sends, recvs):
+        for way, sign in ((0, 1), (1, -1)):
+            q = c - d * sign
+            have = (q >= 0) & (q < cols)
+            more = (c + sign >= 0) & (c + sign < cols)
+
+            def act(q=q, way=way, sign=sign, more=more):
+                copy = remote(at(q), at(q), sends.at[d, way], recvs.at[q], r, c + sign)
+                if d:
+                    copy.wait_recv()
+
+                @pl.when(more)
+                def _():
+                    copy.start()
+
+            if d:
+                pl.when(have)(act)
+            else:
+                act()
+
+    def z_drain(at, sends, recvs):
+        for d in range(cols - 1):
+            for way, sign in ((0, 1), (1, -1)):
+                q = c - d * sign
+                go = (q >= 0) & (q < cols) & (c + sign >= 0) & (c + sign < cols)
+
+                @pl.when(go)
+                def _(q=q, way=way, sign=sign):
+                    remote(at(q), at(q), sends.at[d, way], recvs.at[q], r, c + sign).wait_send()
+
+    def v_at(k):
+        if k < first:
+            return (lambda q: ref["v_one"].at[k, q]), ref["v_send"].at[k], ref["v_recv"].at[k]
+        return (lambda q: ref["v_two"].at[q]), ref["v_send"].at[k], ref["v_recv"].at[k]
+
+    one_rows = ref["v_one"].shape[2]
+    two_rows = ref["v_two"].shape[1]
+    take1 = ones_at(iota((one_rows, entries), 0) == mark1)
+    for k in range(chunks):
+        for rel in (1, 2, 3):
+            gather[k, rel].wait_recv()
+            peer = peers[rel]
+            part = pall.at[k, own_rows(peer)]
+            gather[k, 3 + rel] = launch(
+                remote(part, part, ref["g_send"].at[k, 3 + rel], ref["g_recv"].at[k, 3 + rel], mate)
+            )
+        for rel in (0, 4, 5, 6):
+            gather[k, rel].wait_recv()
+        high, low = halves_of(pall[k])
+        span = slice(k * width, (k + 1) * width)
+        ref["ph"][:, span] = high
+        ref["pl"][:, span] = low
+        take = take1 if k < first else ones_at(iota((two_rows, entries), 0) == mark2)
+        picked = dd(take, high) + dd(take, low)
+        if k < first:
+            ref["v_one"][k, pl.ds(c, 1)] = picked[None]
+        else:
+            ref["v_two"][pl.ds(c, 1)] = picked[None]
+        z_step(0, *v_at(k))
+
+    keep(1, upper2, r_place2)
+    low_spot = spots(iota((128, entries), 0) == lower2, r_place2 - float(tall))
+    spread_low = ones_at(low_spot == iota((128, edge), 1).astype(F32))
+
+    def sizes(k):
+        return wide if k < first else wide + first * width
+
+    block = width * 3 if tiles % 3 == 0 else width
+
+    def unit(k, rel):
+        klass = chip_at(rel)
+        buf = ref[f"z{k}"]
+        if k < first:
+            value = ref["v_one"][k, pl.ds(klass, 1)].reshape(one_rows, width)[:row_slots]
+        else:
+            both = ref["v_two"][pl.ds(klass, 1)].reshape(two_rows, width)
+            value = both[:row_slots]
+            under = halves_of(grown(both[row_slots : row_slots + low_slots], 128).T)
+            under = halves_of(dd(under[0], spread_low) + dd(under[1], spread_low))
+        turned = halves_of(grown(value, row_pad).T)
+        at = 0 if k < first else 1
+
+        def step(j, carry):
+            span = pl.ds(pl.multiple_of(j * block, 128), block)
+            kept = (ref["kept_h"][at, :, span], ref["kept_l"][at, :, span])
+            out = three(turned, kept)
+            if k >= first:
+                out = out - three(under, (ref["y_h"][:edge, span], ref["y_l"][:edge, span]))
+            buf[rel, 0, :, span] = out[:height]
+            buf[rel, 1, :, span] = out[height:]
+            return carry
+
+        lax.fori_loop(0, wide // block, step, 0)
+        if k >= first:
+            out = three(under, (ref["d_h"][...], ref["d_l"][...]))
+            buf[rel, 0, :, wide:] = out[:height]
+            buf[rel, 1, :, wide:] = out[height:]
+        return launch(
+            remote(
+                buf.at[rel, 1 - core],
+                ref[f"m{k}"].at[rel],
+                ref["r_send"].at[k, rel],
+                ref["r_recv"].at[k, rel],
+                mate,
+            )
+        )
+
+    def strips(count, body):
+        def step(i, carry):
+            body(pl.multiple_of(i * 8, 8))
+            return carry
+
+        lax.fori_loop(0, count // 8, step, 0)
+
+    def begin(k):
+        swaps = {rel: unit(k, rel) for rel in (3, 1, 2, 0)}
+        total = ref[f"t{k}"]
+        buf = ref[f"z{k}"]
+        got = ref[f"m{k}"]
+        live = {}
+
+        def pair(rel):
+            swaps[rel].wait_recv()
+
+            def body(i):
+                at = pl.ds(i, 8)
+                mine = buf[rel, pl.ds(core, 1), at, :].reshape(8, sizes(k))
+                total[rel, at, :] = mine + got[rel, at, :]
+
+            strips(height, body)
+
+        def pass_on(index, source, target, peer):
+            live[index] = launch(
+                remote(source, target, ref["r_send"].at[k, index], ref["r_recv"].at[k, index], peer)
+            )
+
+        lower = pl.ds(0, half)
+        upper = pl.ds(half, half)
+        pair(3)
+        pass_on(4, total.at[3, lower], ref[f"i{k}"].at[0], by_x)
+        pass_on(5, total.at[3, upper], ref[f"i{k}"].at[1], by_y)
+        pair(1)
+        pass_on(6, total.at[1, lower], ref[f"f{k}"].at[0], by_x)
+        pair(2)
+        pass_on(7, total.at[2, upper], ref[f"f{k}"].at[1], by_y)
+        return swaps, live, pass_on
+
+    def middle(k, state):
+        swaps, live, pass_on = state
+        total = ref[f"t{k}"]
+        live[5].wait_recv()
+
+        def body(i):
+            at = pl.ds(pl.multiple_of(i + half, 8), 8)
+            total[1, at, :] = total[1, at, :] + ref[f"i{k}"][1, pl.ds(i, 8), :]
+
+        strips(half, body)
+        pass_on(8, total.at[1, pl.ds(half, half)], ref[f"f{k}"].at[2], by_x)
+        live[4].wait_recv()
+
+        def body(i):
+            at = pl.ds(i, 8)
+            total[2, at, :] = total[2, at, :] + ref[f"i{k}"][0, at, :]
+
+        strips(half, body)
+        pass_on(9, total.at[2, pl.ds(0, half)], ref[f"f{k}"].at[3], by_y)
+
+    def finish(k, state):
+        swaps, live, pass_on = state
+        swaps[0].wait_recv()
+        for index in (6, 7, 8, 9):
+            live[index].wait_recv()
+        buf = ref[f"z{k}"]
+        got = ref[f"m{k}"]
+        fin = ref[f"f{k}"]
+        out = ref[f"t{k}"]
+        for start, one, two in ((0, 0, 3), (half, 1, 2)):
+
+            def body(i, start=start, one=one, two=two):
+                at = pl.ds(pl.multiple_of(i + start, 8), 8)
+                own = buf[0, pl.ds(core, 1), at, :].reshape(8, sizes(k)) + got[0, at, :]
+                out[0, at, :] = own + (fin[one, pl.ds(i, 8), :] + fin[two, pl.ds(i, 8), :])
+
+            strips(half, body)
+
+        rows_at = pl.ds(k * height, height)
+
+        def step(j, carry):
+            span = pl.ds(pl.multiple_of(j * width, 128), width)
+            tile = out[0, :, span]
+            high, low = halves_of(tile)
+            ref["y_h"][rows_at, span] = high
+            ref["y_l"][rows_at, span] = low
+            if k < first:
+                ref["out_one"][k, pl.ds(j, 1)] = -tile[None]
+            else:
+                ref["out_two"][0, pl.ds(j, 1)] = -tile[None]
+            return carry
+
+        lax.fori_loop(0, tiles, step, 0)
+
+    for k in range(first):
+        for kk in range(first):
+            high, low = halves_of(ref["diag_one"][k, kk])
+            ref["d_h"][k * height : (k + 1) * height, kk * width : (kk + 1) * width] = high
+            ref["d_l"][k * height : (k + 1) * height, kk * width : (kk + 1) * width] = low
+
+    def arrive(at, steps):
+        for d in steps:
+            z_step(d, *at)
+
+    every = range(1, cols)
+    states = []
+    for k in range(first):
+        arrive(v_at(k), every)
+        states.append(begin(k))
+        middle(k, states[k])
+    arrive(v_at(first), every)
+    for k in range(first):
+        finish(k, states[k])
+
+    def picker(owner, slot, place, extra=None):
+        mine = owner == c
+        if extra is not None:
+            mine = mine & extra
+        spot = spots(iota((col_slots, entries), 0) == jnp.where(mine, slot, -1), place)
+        return ones_at(spot == iota((col_slots, wide), 1).astype(F32))
+
+    ref["pick"][0] = picker(c_owner1, c_slot1, c_place1)
+    ref["pick"][1] = picker(c_owner2, c_slot2, c_place2, above)
+
+    def s_at(n):
+        return (lambda q: ref["s"].at[n, q]), ref["s_send"].at[n], ref["s_recv"].at[n]
+
+    pick1 = ref["pick"][0]
+    chosen = dd(pick1, ref["y_h"][:edge], 1, 1) + dd(pick1, ref["y_l"][:edge], 1, 1)
+    ref["s"][0, pl.ds(c, 1)] = chosen[None]
+    z_step(0, *s_at(0))
+    last = begin(first)
+    z_step(1, *s_at(0))
+
+    def order_one(q, carry):
+        take = ones_at(iota((col_pad, entries), 0) == jnp.where(c_owner1 == q, c_slot1, -1))
+        ref["c1_h"][pl.ds(q, 1)] = dd(take, ref["ph"][:, : first * width]).astype(BF16)[None]
+        ref["c1_l"][pl.ds(q, 1)] = dd(take, ref["pl"][:, : first * width]).astype(BF16)[None]
+        return carry
+
+    lax.fori_loop(0, cols, order_one, 0)
+    middle(first, last)
+    z_step(2, *s_at(0))
+
+    def order_two(q, carry):
+        mark = jnp.where((c_owner2 == q) & above, c_slot2, -1)
+        take = ones_at(iota((col_pad, entries), 0) == mark)
+        ref["c2_h"][pl.ds(q, 1)] = dd(take, ref["ph"][:, first * width :]).astype(BF16)[None]
+        ref["c2_l"][pl.ds(q, 1)] = dd(take, ref["pl"][:, first * width :]).astype(BF16)[None]
+        place = (over(row2, TILE) - tiles) * width + within(row2, width)
+        mark = jnp.where((c_owner2 != q) | above, -1, place)
+        take = ones_at(iota((first * width, entries), 0) == mark)
+        ref["cl_h"][pl.ds(q, 1)] = dd(take, ref["ph"][:, first * width :]).astype(BF16)[None]
+        ref["cl_l"][pl.ds(q, 1)] = dd(take, ref["pl"][:, first * width :]).astype(BF16)[None]
+        return carry
+
+    lax.fori_loop(0, cols, order_two, 0)
+    finish(first, last)
+    tail_h = ref["y_h"][edge:]
+    tail_l = ref["y_l"][edge:]
+    none = jnp.zeros_like(tail_h)
+    pick1 = ref["pick"][0]
+    pick2 = ref["pick"][1]
+    chosen = (
+        dd(pick1, jnp.concatenate([tail_h, none], axis=0), 1, 1)
+        + dd(pick1, jnp.concatenate([tail_l, none], axis=0), 1, 1)
+        + dd(pick2, jnp.concatenate([none, tail_h], axis=0), 1, 1)
+        + dd(pick2, jnp.concatenate([none, tail_l], axis=0), 1, 1)
+    )
+    ref["s"][1, pl.ds(c, 1)] = chosen[None]
+    z_step(0, *s_at(1))
+    z_step(3, *s_at(0)) if cols > 3 else None
+    z_step(1, *s_at(1))
+
+    def turned(n, q):
+        return halves_of(grown(ref["s"][n, q], col_pad).T)
+
+    corner = jnp.zeros((edge, first * width), F32)
+    for q in range(cols):
+        corner = corner + three(turned(0, q), (ref["c1_h"][q], ref["c1_l"][q]))
+    for k in range(first):
+        for kk in range(first):
+            piece = corner[k * height : (k + 1) * height, kk * width : (kk + 1) * width]
+            ref["out_one"][k, tiles + kk] = ref["diag_one"][k, kk] + piece
+    arrive(s_at(1), range(2, cols))
+    cross = jnp.zeros((2 * height, first * width), F32)
+    final = jnp.zeros((2 * height, width), F32)
+    for q in range(cols):
+        both = turned(1, q)
+        cross = cross + three(both, (ref["c1_h"][q], ref["c1_l"][q]))
+        final = final + three(both, (ref["c2_h"][q], ref["c2_l"][q]))
+    bottom = cross[:height] - ref[f"t{first}"][0, :, wide:]
+    ref["b"][pl.ds(c, 1)] = bottom[None]
+    ends = []
+    for step in range(1, cols):
+        other = (c + step) % cols
+        ends.append(
+            launch(
+                remote(
+                    ref["b"].at[c], ref["b"].at[c], ref["b_send"].at[step], ref["b_recv"].at[c], r, other
+                )
+            )
+        )
+    for kk in range(first):
+        ref["out_two"][0, tiles + kk] = bottom[:, kk * width : (kk + 1) * width]
+    for step in range(1, cols):
+        other = (c + step) % cols
+        remote(
+            ref["b"].at[other], ref["b"].at[other], ref["b_send"].at[step], ref["b_recv"].at[other], r, other
+        ).wait_recv()
+    result = ref["diag_two"][0, 0] + final[height:]
+    for q in range(cols):
+        result = result - three(halves_of(ref["b"][q]), (ref["cl_h"][q], ref["cl_l"][q]))
+    ref["out_two"][0, tiles + first] = result
+
+    for _, copy in sent:
+        copy.wait_send()
+    for k in range(chunks):
+        z_drain(*v_at(k))
+    for n in range(2):
+        z_drain(*s_at(n))
+
+
+def on_device_fused(
+    ancestor,
+    inverse_first,
+    panel_first,
+    structure_first,
+    inverse_second,
+    panel_second,
+    structure_second,
+):
+    rows = lax.axis_size("row")
+    cols = lax.axis_size("col")
+    height = TILE // rows
+    width = TILE // cols
+    tiles = ancestor.shape[0]
+    first = inverse_first.shape[0]
+    entries = structure_first.shape[0]
+    chunks = first + 1
+    wide = tiles * width
+    tall = tiles * height
+    row_slots = tall // GRAIN * CAP
+    low_slots = first * height // GRAIN * CAP
+    col_slots = wide // GRAIN * CAP
+    row_pad = -(-row_slots // 128) * 128
+    col_pad = -(-col_slots // 128) * 128
+    one_rows = -(-row_slots // 16) * 16
+    two_rows = -(-(row_slots + low_slots) // 16) * 16
+    panel = jnp.concatenate([panel_first.transpose(1, 0, 2), panel_second.transpose(1, 0, 2)], axis=0)
+    structure = jnp.stack([structure_first, structure_second])
+    dma = pltpu.SemaphoreType.DMA
+    scratch = {
+        "pall": pltpu.VMEM((chunks, entries, width), F32),
+        "ph": pltpu.VMEM((entries, chunks * width), BF16),
+        "pl": pltpu.VMEM((entries, chunks * width), BF16),
+        "kept_h": pltpu.VMEM((2, row_pad, wide), BF16),
+        "kept_l": pltpu.VMEM((2, row_pad, wide), BF16),
+        "v_one": pltpu.VMEM((first, cols, one_rows, width), F32),
+        "v_two": pltpu.VMEM((cols, two_rows, width), F32),
+        "y_h": pltpu.VMEM((chunks * height, wide), BF16),
+        "y_l": pltpu.VMEM((chunks * height, wide), BF16),
+        "d_h": pltpu.VMEM((first * height, first * width), BF16),
+        "d_l": pltpu.VMEM((first * height, first * width), BF16),
+        "pick": pltpu.VMEM((2, col_slots, wide), BF16),
+        "s": pltpu.VMEM((2, cols, col_slots, 2 * height), F32),
+        "c1_h": pltpu.VMEM((cols, col_pad, first * width), BF16),
+        "c1_l": pltpu.VMEM((cols, col_pad, first * width), BF16),
+        "c2_h": pltpu.VMEM((cols, col_pad, width), BF16),
+        "c2_l": pltpu.VMEM((cols, col_pad, width), BF16),
+        "cl_h": pltpu.VMEM((cols, first * width, width), BF16),
+        "cl_l": pltpu.VMEM((cols, first * width, width), BF16),
+        "b": pltpu.VMEM((cols, height, first * width), F32),
+        "g_send": dma((chunks, 7)),
+        "g_recv": dma((chunks, 7)),
+        "v_send": dma((chunks, cols, 2)),
+        "v_recv": dma((chunks, cols)),
+        "r_send": dma((chunks, 10)),
+        "r_recv": dma((chunks, 10)),
+        "s_send": dma((2, cols, 2)),
+        "s_recv": dma((2, cols)),
+        "b_send": dma((cols,)),
+        "b_recv": dma((cols,)),
+    }
+    for k in range(chunks):
+        size = wide if k < first else wide + first * width
+        scratch[f"z{k}"] = pltpu.VMEM((4, 2, height, size), F32)
+        scratch[f"m{k}"] = pltpu.VMEM((4, height, size), F32)
+        scratch[f"t{k}"] = pltpu.VMEM((4, height, size), F32)
+        scratch[f"i{k}"] = pltpu.VMEM((2, height // 2, size), F32)
+        scratch[f"f{k}"] = pltpu.VMEM((4, height // 2, size), F32)
+    inputs = ["ancestor", "diag_one", "diag_two", "panel", "srow", "scol"]
+    names = inputs + ["out_one", "out_two"] + list(scratch)
+    vmem = pl.BlockSpec(memory_space=pltpu.VMEM)
+    dims = (rows, cols, height, width, tiles, first, entries)
+    return pl.pallas_call(
+        functools.partial(fused, dims, names),
+        out_shape=(
+            jax.ShapeDtypeStruct((first, tiles + first, height, width), F32),
+            jax.ShapeDtypeStruct((1, tiles + first + 1, height, width), F32),
+        ),
+        in_specs=[vmem] * len(inputs),
+        out_specs=(vmem, vmem),
+        scratch_shapes=list(scratch.values()),
+        compiler_params=pltpu.CompilerParams(
+            collective_id=0, has_side_effects=True, vmem_limit_bytes=60 * 1024 * 1024
+        ),
+    )(
+        open_packed(ancestor, height, width),
+        open_packed(inverse_first, height, width),
+        open_packed(inverse_second, height, width),
+        panel,
+        structure,
+        structure.T,
+    )
+
+
+def fits(rows, cols):
+    return rows == 8 and rows == 2 * cols and TILE // cols % 128 == 0
+
 
 def solution(mesh):
+    body = on_device_fused if fits(mesh.shape["row"], mesh.shape["col"]) else on_device
     in_specs = (
         P(None, None, "row", "col"),
         P(None, None, "row", "col"),
@@ -225,5 +839,5 @@
     )
     out_specs = (P(None, None, "row", "col"), P(None, None, "row", "col"))
     return jax.shard_map(
-        on_device, mesh=mesh, in_specs=in_specs, out_specs=out_specs, check_vma=False
-    )
+        body, mesh=mesh, in_specs=in_specs, out_specs=out_specs, check_vma=False
+    )

time: 280 us -> 119 us (0.42); the launches traced: 275 us -> 119 us
  waiting for transfers between devices: 164 us -> 0 us
  Pallas kernels: 0 us -> 109 us
  matrix products: 35.5 us -> 0 us
  local copies, waits for them, and re-layouts: 27.7 us -> 7.34 us
  other arithmetic: 18.6 us -> 1.64 us
  blocking collectives: 14.1 us -> 0 us
  between operations: 14.5 us -> 0.66 us
    pallas_call x0 -> x1, Pallas kernels: none -> 109 us  [on_device_fused(): pl.pallas_call(functools.partial(fused, dims, names), out_shape=(jax.Shap...]
    all_gather x3 -> x0, waiting for transfers between devices: 96.3 us -> none  [the longest x1 39.3 us: on_device(): lax.all_gather(jnp.concatenate([part_first, part_second], axis=0), 'col',...]
    reduce_scatter x1 -> x0, waiting for transfers between devices: 67.3 us -> none  [on_device(): summed = lax.psum_scatter(joined, 'row', scatter_dimension=0, tiled=False)]
    dot_general x16 -> x0, matrix products: 35.5 us -> none  [product(): lax.dot_general(left, right, (((left_dim,), (0,)), ((), ())), precision=l...]
    all_gather x1 -> x0, blocking collectives: 14.1 us -> none  [on_device(): low_all = lax.all_gather(low_block, 'col', axis=0)]
    slice x11 -> x0, local copies, waits for them, and re-layouts: 9.2 us -> none  [the longest x1 2.4 us: on_device(): spread[:, cut:].reshape(cols, row_slots + low_slots, halves, second, height)]
    concatenate x7 -> x1, other arithmetic: 7.48 us -> 1.63 us  [on_device_fused(): jnp.concatenate([panel_first.transpose(1, 0, 2), panel_second.transpose(1...]
    reduce_sum x2 -> x0, other arithmetic: 5.33 us -> none  [entry_ranks(): return jnp.sum(same.astype(jnp.int32), axis=1)]
  transfers between devices with their start and end apart: 4 -> 0, of which waited for: 4 -> 0; matrix products, arithmetic and copies ran while one was open for 10% -> 0% of each run, Pallas kernels for 0% -> 0%
where the time goes in v1:
time: 119 us
  Pallas kernels  109 us (92%)
  local copies, waits for them, and re-layouts  7.34 us (6%)
  other arithmetic  1.64 us (1%)
    pallas_call x1, Pallas kernels, on_device_fused(): pl.pallas_call(functools.partial(fused, dims, names), out_shape=(jax.Shap...  109 us
    unnamed x5, local copies, waits for them, and re-layouts  4.76 us
    another operation x3, local copies, waits for them, and re-layouts, on_device_fused(): structure = jnp.stack([structure_first, structure_second])  2.59 us

profile of v1, /device:TPU:0, one launch (start us, length us, event | category | flops | bytes accessed | tf_op | source)
XLA Modules:
  0.0 118.8 jit_solution(6197548930817894529)
XLA Ops:
  0.6 0.7 stack.9
  1.3 0.7 stack.10
  2.0 0.0 copy-start
  2.1 0.9 copy.18
  3.0 1.6 %pad_maximum_fusion.refs_3_ = f32[3,192,128]{2,1,0:T(8,128)} fusion(f32[1,192,128]{2,1,0:T(8,128)} %bitcast.7, f32[2,192,128]{2,1,0:T(8,128)S(1)} %bitcast.6), kind=kLoop, calls=%fused_computation | loop fusion | flops 73728 | bytes 589824 | tf_op jit(solution)/shard_map/concatenate | solution.py:757
  4.6 1.2 copy.16
  5.8 0.0 copy-done
  5.8 109.1 %shard_map.86 = (f32[2,11,64,128]{3,2,1,0:T(8,128)}, f32[1,12,64,128]{3,2,1,0:T(8,128)}) custom-call(f32[9,9,64,128]{3,2,1,0:T(8,128)} %refs_0_.1, f32[2,2,64,128]{3,2,1,0:T(8,128)} %refs_1_.1, f32[1,1,64,128]{3,2,1,0:T(8,128)} %refs_2_.1, f32[3,192,128]{2,1,0:T(8,128)} %pad_maximum_fusion.refs_3_, s32[2,1536]{1,0:T(2,128)} %copy-done, s32[1536,2]{1,0:T(8,128)} %bitcast.5), custom_call_target="tpu_custom_call" | custom-call | tf_op jit(solution)/shard_map/pallas_call | solution.py:803
  114.9 2.0 %copy.21 = f32[2,11,64,128]{3,2,1,0:T(8,128)} copy(f32[2,11,64,128]{3,2,1,0:T(8,128)} %get-tuple-element.4) | data formatting | bytes 1441792
  117.0 1.8 %copy.22 = f32[1,12,64,128]{3,2,1,0:T(8,128)} copy(f32[1,12,64,128]{3,2,1,0:T(8,128)} %get-tuple-element.5) | data formatting | bytes 786432
  (1 shorter events, 0.0 us)
Async XLA Ops:
  2.0 3.8 %copy-start = (s32[2,1536]{1,0:T(2,128)}, s32[2,1536]{1,0:T(2,128)S(1)}, u32[]{:S(2)}) copy-start(s32[2,1536]{1,0:T(2,128)S(1)} %pad_add_fusion.refs_4_) | copy-start | bytes 36868

commit v2 on v0

--- a/solution.py
+++ b/solution.py
@@ -1,6 +1,10 @@
+import functools
+
 import jax
 import jax.numpy as jnp
 from jax import lax
+from jax.experimental import pallas as pl
+from jax.experimental.pallas import tpu as pltpu
 from jax.sharding import PartitionSpec as P
 
 TILE = 512
@@ -212,8 +216,700 @@
     )
     return (close_packed(row_first), close_packed(row_second))
 
+F32 = jnp.float32
+BF16 = jnp.bfloat16
+MESH = pl.DeviceIdType.MESH
+
+
+def over(value, size):
+    return lax.shift_right_logical(value, jnp.int32(size.bit_length() - 1))
+
+
+def within(value, size):
+    return value & jnp.int32(size - 1)
+
+
+def iota(shape, dim):
+    return lax.broadcasted_iota(jnp.int32, shape, dim)
+
+
+def ones_at(mask):
+    return jnp.where(mask, 1.0, 0.0).astype(BF16)
+
+
+def dd(left, right, left_dim=1, right_dim=0):
+    return lax.dot_general(
+        left, right, (((left_dim,), (right_dim,)), ((), ())), preferred_element_type=F32
+    )
+
+
+def halves_of(value):
+    high = value.astype(BF16)
+    return high, (value - high.astype(F32)).astype(BF16)
+
+
+def three(left, right):
+    return dd(left[0], right[0]) + dd(left[0], right[1]) + dd(left[1], right[0])
+
+
+def grown(value, count):
+    rest = count - value.shape[0]
+    return jnp.concatenate([value, jnp.zeros((rest, value.shape[1]), value.dtype)], axis=0)
+
+
+def spots(hits, places):
+    return jnp.max(jnp.where(hits, places, -1.0), axis=1, keepdims=True)
+
+
+def fused(dims, names, *refs):
+    ref = dict(zip(names, refs))
+    rows, cols, height, width, tiles, first, entries, groups = dims
+    chunks = first + 1
+    shard = entries // rows
+    wide = tiles * width
+    tall = tiles * height
+    row_slots = tall // GRAIN * CAP
+    low_slots = first * height // GRAIN * CAP
+    tile_slots = width // GRAIN * CAP
+    col_slots = tiles * tile_slots
+    edge = first * height
+    fringe = first * width
+    row_pad = -(-row_slots // 128) * 128
+    col_pad = -(-col_slots // 128) * 128
+    half = height // 2
+
+    r = lax.axis_index("row")
+    c = lax.axis_index("col")
+    core = r % 2
+    chip = r // 2
+    chip_x = chip % 2
+    chip_y = chip // 2
+    by_x = r + 2 - 4 * chip_x
+    by_y = r + 4 - 8 * chip_y
+    by_both = r + 6 - 4 * chip_x - 8 * chip_y
+    mate = r + 1 - 2 * core
+    peers = {3: by_both, 1: by_x, 2: by_y}
+
+    def chip_at(rel):
+        x = 1 - chip_x if rel % 2 else chip_x
+        y = 1 - chip_y if rel // 2 else chip_y
+        return y * 2 + x
+
+    sent = []
+    drains = []
+
+    def remote(source, target, send, recv, device, column=None):
+        return pltpu.make_async_remote_copy(
+            src_ref=source,
+            dst_ref=target,
+            send_sem=send,
+            recv_sem=recv,
+            device_id=(device, c if column is None else column),
+            device_id_type=MESH,
+        )
+
+    def launch(copy):
+        copy.start()
+        sent.append(copy)
+        return copy
+
+    barrier = pltpu.get_barrier_semaphore()
+    for peer in (mate, by_x, by_y, by_both):
+        pl.semaphore_signal(barrier, inc=1, device_id=(peer, c), device_id_type=MESH)
+    for step in range(1, cols):
+        other = (c + step) % cols
+        pl.semaphore_signal(barrier, inc=1, device_id=(r, other), device_id_type=MESH)
+    loads = []
+    for index, (source, target) in enumerate(
+        (("ancestor", "a"), ("diag_one", "d_one"), ("diag_two", "d_two"))
+    ):
+        loads.append(pltpu.make_async_copy(ref[source], ref[target], ref["l_sem"].at[index]))
+        loads[-1].start()
+
+    def ranks(row):
+        group = over(row, GRAIN)
+        total = [jnp.zeros((1, 128), F32) for _ in range(entries // 128)]
+        lanes = iota((128, 128), 1)
+        order = iota((128, 128), 0)
+        for b in range(entries // 128):
+            one = group[:, b * 128 : (b + 1) * 128]
+            column = jnp.broadcast_to(one, (128, 128)).T
+            for t in range(b, entries // 128):
+                hit = column == group[:, t * 128 : (t + 1) * 128]
+                if t == b:
+                    hit = hit & (order < lanes)
+                total[t] = total[t] + jnp.sum(jnp.where(hit, 1.0, 0.0), axis=0, keepdims=True)
+        return jnp.concatenate(total, axis=1).astype(jnp.int32)
+
+    def owned(row, rank, size):
+        owner = over(within(row, TILE), size)
+        group = over(row, TILE) * (size // GRAIN) + over(within(row, size), GRAIN)
+        place = over(row, TILE) * size + within(row, size)
+        return owner, group * CAP + rank, place.astype(F32)
+
+    row1 = ref["list_one"][...].reshape(1, entries)
+    row2 = ref["list_two"][...].reshape(1, entries)
+    rank1 = ranks(row1)
+    rank2 = ranks(row2)
+    above = row2 < tiles * TILE
+    r_owner1, r_slot1, r_place1 = owned(row1, rank1, height)
+    r_owner2, r_slot2, r_place2 = owned(row2, rank2, height)
+    c_owner1, c_slot1, c_place1 = owned(row1, rank1, width)
+    c_owner2, c_slot2, c_place2 = owned(row2, rank2, width)
+    mark1 = jnp.where(r_owner1 == r, r_slot1, -1)
+    mark2 = jnp.where(r_owner2 == r, r_slot2, -1)
+    upper2 = jnp.where(above, mark2, -1)
+    lower2 = jnp.where(above | (r_owner2 != r), -1, r_slot2 - row_slots)
+
+    pl.semaphore_wait(barrier, 4 + cols - 1)
+    pall = ref["pall"]
+
+    def own_rows(device):
+        return pl.ds(pl.multiple_of(device * shard, 8), shard)
+
+    def panel(k):
+        return ref["panel_one"].at[k] if k < first else ref["panel_two"].at[k - first]
+
+    gather = {}
+    for k in range(chunks):
+        for rel, peer in (*peers.items(), (0, mate)):
+            gather[k, rel] = launch(
+                remote(
+                    panel(k),
+                    pall.at[k, own_rows(r)],
+                    ref["g_send"].at[k, rel],
+                    ref["g_recv"].at[k, rel],
+                    peer,
+                )
+            )
+    for k in range(chunks):
+        pall[k, own_rows(r), :] = panel(k)[...]
+
+    def keep(at, marks, places):
+        spot = spots(iota((row_pad, entries), 0) == marks, places)
+        take = ones_at(spot == iota((row_pad, tall), 1).astype(F32))
+
+        def step(j, carry):
+            block = ref["a"][:, pl.ds(j, 1), :, :].reshape(tall, width)
+            high, low = halves_of(block)
+            span = pl.ds(pl.multiple_of(j * width, 128), width)
+            ref["kept_h"][at, :, span] = dd(take, high).astype(BF16)
+            ref["kept_l"][at, :, span] = dd(take, low).astype(BF16)
+            return carry
+
+        lax.fori_loop(0, tiles, step, 0)
+
+    def spread(at, sends, recvs):
+        for index, (sign, reach) in enumerate(((1, 2), (-1, 2), (1, 1), (-1, 1))):
+            there = c + sign * reach
+            go = (there >= 0) & (there < cols)
+
+            def copy(there=there, index=index):
+                return remote(at(c), at(c), sends.at[index], recvs.at[c], r, there)
+
+            @pl.when(go)
+            def _(copy=copy):
+                copy().start()
+
+            drains.append((go, copy))
+
+    def forward(at, sends, recvs):
+        for index, sign in ((4, 1), (5, -1)):
+            q = c - 2 * sign
+            there = c + sign
+            go = (q >= 0) & (q < cols) & (there >= 0) & (there < cols)
+
+            def copy(q=q, there=there, index=index):
+                return remote(at(q), at(q), sends.at[index], recvs.at[q], r, there)
+
+            @pl.when(go)
+            def _(copy=copy):
+                copy().wait_recv()
+                copy().start()
+
+            drains.append((go, copy))
+
+    def arrive(at, sends, recvs):
+        for reach in range(1, cols):
+            for sign in (1, -1):
+                q = c - reach * sign
+                there = c + sign
+                go = (q >= 0) & (q < cols)
+                if reach == 2:
+                    go = go & ((there < 0) | (there >= cols))
+
+                @pl.when(go)
+                def _(q=q):
+                    remote(at(q), at(q), sends.at[0], recvs.at[q], r, c).wait_recv()
+
+    def v_at(k):
+        if k < first:
+            return (lambda q: ref["v_one"].at[k, q]), ref["v_send"].at[k], ref["v_recv"].at[k]
+        return (lambda q: ref["v_two"].at[q]), ref["v_send"].at[k], ref["v_recv"].at[k]
+
+    one_rows = -(-row_slots // 16) * 16
+    two_rows = -(-(row_slots + low_slots) // 16) * 16
+    take1 = ones_at(iota((one_rows, entries), 0) == mark1)
+    loads[0].wait()
+    keep(0, mark1, r_place1)
+    for k in range(chunks):
+        for rel in (1, 2, 3):
+            gather[k, rel].wait_recv()
+            part = pall.at[k, own_rows(peers[rel])]
+            gather[k, 3 + rel] = launch(
+                remote(part, part, ref["g_send"].at[k, 3 + rel], ref["g_recv"].at[k, 3 + rel], mate)
+            )
+        for rel in (0, 4, 5, 6):
+            gather[k, rel].wait_recv()
+        high, low = halves_of(pall[k])
+        span = slice(k * width, (k + 1) * width)
+        ref["ph"][:, span] = high
+        ref["pl"][:, span] = low
+        take = take1 if k < first else ones_at(iota((two_rows, entries), 0) == mark2)
+        picked = dd(take, high) + dd(take, low)
+        if k < first:
+            ref["v_one"][k, pl.ds(c, 1)] = picked[None, :row_slots]
+        else:
+            ref["v_two"][pl.ds(c, 1)] = picked[None, : row_slots + low_slots]
+        spread(*v_at(k))
+        if k:
+            forward(*v_at(k - 1))
+
+    keep(1, upper2, r_place2)
+    low_spot = spots(iota((128, entries), 0) == lower2, r_place2 - float(tall))
+    spread_low = ones_at(low_spot == iota((128, edge), 1).astype(F32))
+    for load in loads[1:]:
+        load.wait()
+    for k in range(first):
+        for kk in range(first):
+            high, low = halves_of(ref["d_one"][k, kk])
+            ref["d_h"][k * height : (k + 1) * height, kk * width : (kk + 1) * width] = high
+            ref["d_l"][k * height : (k + 1) * height, kk * width : (kk + 1) * width] = low
+
+    def picker(which, owner, slot, place, extra=None):
+        mine = owner == c
+        if extra is not None:
+            mine = mine & extra
+        spot = spots(iota((col_slots, entries), 0) == jnp.where(mine, slot, -1), place)
+        for start, stop in groups:
+            span = slice(start * tile_slots, stop * tile_slots)
+            count = (stop - start) * width
+            here = iota(((stop - start) * tile_slots, count), 1) + start * width
+            ref["pick"][which, span, :count] = ones_at(spot[span] == here.astype(F32))
+
+    picker(0, c_owner1, c_slot1, c_place1)
+    picker(1, c_owner2, c_slot2, c_place2, above)
+
+    def ready(k):
+        arrive(*v_at(k))
+        for rel in range(4):
+            klass = chip_at(rel)
+            if k < first:
+                value = ref["v_one"][k, pl.ds(klass, 1)].reshape(row_slots, width)
+            else:
+                both = ref["v_two"][pl.ds(klass, 1)].reshape(row_slots + low_slots, width)
+                value = both[:row_slots]
+                under = halves_of(grown(both[row_slots:], 128).T)
+                under = halves_of(dd(under[0], spread_low) + dd(under[1], spread_low))
+                for n in range(2):
+                    start = (4 * n + rel) * width
+                    ref["under"][start : start + width, :] = under[n]
+            turned = halves_of(grown(value, row_pad).T)
+            for n in range(2):
+                start = (4 * n + rel) * width
+                ref["turned"][k, start : start + width, :] = turned[n]
+
+    def stacked(left, high, low):
+        count = left.shape[0] // 2
+        both = dd(left, high)
+        return both[:count] + both[count:] + dd(left[:count], low)
+
+    stages = [(k, g) for g in range(len(groups)) for k in range(first)]
+    stages += [(first, g) for g in range(len(groups))]
+    names_of = {stage: s for s, stage in enumerate(stages)}
+    live = {}
+
+    def put(s, part, start, stop):
+        for rel in range(4):
+            for side in range(2):
+                top = rel * width + side * height
+                ref[f"z{s}"][side, rel, :, start:stop] = part[top : top + height]
+
+    def begin(s):
+        k, g = stages[s]
+        start, stop = groups[g]
+        span = slice(start * width, stop * width)
+        count = (stop - start) * width
+        at = 0 if k < first else 1
+        part = stacked(ref["turned"][k], ref["kept_h"][at, :, span], ref["kept_l"][at, :, span])
+        if k >= first:
+            part = part - stacked(ref["under"][...], ref["y_h"][:edge, span], ref["y_l"][:edge, span])
+        put(s, part, 0, count)
+        if k >= first and g == len(groups) - 1:
+            part = stacked(ref["under"][...], ref["d_h"][...], ref["d_l"][...])
+            put(s, part, count, count + fringe)
+        live[s, 0] = launch(
+            remote(
+                ref[f"z{s}"].at[1 - core],
+                ref[f"m{s}"],
+                ref["r_send"].at[s, 0],
+                ref["r_recv"].at[s, 0],
+                mate,
+            )
+        )
+
+    def strips(count, body):
+        def step(i, carry):
+            body(pl.multiple_of(i * 8, 8))
+            return carry
+
+        lax.fori_loop(0, count // 8, step, 0)
+
+    def pass_on(s, index, source, target, peer):
+        live[s, index] = launch(
+            remote(source, target, ref["r_send"].at[s, index], ref["r_recv"].at[s, index], peer)
+        )
+
+    lower = pl.ds(0, half)
+    upper = pl.ds(half, half)
+
+    def push(s):
+        live[s, 0].wait_recv()
+        total = ref[f"t{s}"]
+        got = ref[f"m{s}"]
+        own = ref[f"z{s}"]
+        count = total.shape[2]
+
+        def pair(rel):
+            def body(i):
+                at = pl.ds(i, 8)
+                mine = own[pl.ds(core, 1), rel, at, :].reshape(8, count)
+                total[rel, at, :] = mine + got[rel, at, :]
+
+            strips(height, body)
+
+        pair(3)
+        pass_on(s, 1, total.at[3, lower], ref[f"i{s}"].at[0], by_x)
+        pass_on(s, 2, total.at[3, upper], ref[f"i{s}"].at[1], by_y)
+        pair(1)
+        pass_on(s, 3, total.at[1, lower], ref[f"f{s}"].at[0], by_x)
+        pair(2)
+        pass_on(s, 4, total.at[2, upper], ref[f"f{s}"].at[1], by_y)
+        pair(0)
+
+    def middle(s):
+        total = ref[f"t{s}"]
+        live[s, 2].wait_recv()
+
+        def body(i):
+            at = pl.ds(pl.multiple_of(i + half, 8), 8)
+            total[1, at, :] = total[1, at, :] + ref[f"i{s}"][1, pl.ds(i, 8), :]
+
+        strips(half, body)
+        pass_on(s, 5, total.at[1, upper], ref[f"f{s}"].at[2], by_x)
+        live[s, 1].wait_recv()
+
+        def body(i):
+            at = pl.ds(i, 8)
+            total[2, at, :] = total[2, at, :] + ref[f"i{s}"][0, at, :]
+
+        strips(half, body)
+        pass_on(s, 6, total.at[2, lower], ref[f"f{s}"].at[3], by_y)
+
+    writes = []
+
+    def write(source, target):
+        copy = pltpu.make_async_copy(source, target, ref["w_sem"].at[len(writes)])
+        copy.start()
+        writes.append(copy)
+
+    def s_at(n, g):
+        start, stop = groups[g]
+        span = pl.ds(start * tile_slots, (stop - start) * tile_slots)
+        return (lambda q: ref["s"].at[n, q, span]), ref["s_send"].at[n, g], ref["s_recv"].at[n, g]
+
+    def choose(n, g):
+        start, stop = groups[g]
+        span = slice(start * tile_slots, stop * tile_slots)
+        count = (stop - start) * width
+        columns = slice(start * width, stop * width)
+        pick1 = ref["pick"][0, span, :count]
+        if n == 0:
+            chosen = dd(pick1, ref["y_h"][:edge, columns], 1, 1)
+            chosen = chosen + dd(pick1, ref["y_l"][:edge, columns], 1, 1)
+        else:
+            pick2 = ref["pick"][1, span, :count]
+            high = ref["y_h"][edge:, columns]
+            low = ref["y_l"][edge:, columns]
+            none = jnp.zeros_like(high)
+            chosen = (
+                dd(pick1, jnp.concatenate([high, none], axis=0), 1, 1)
+                + dd(pick1, jnp.concatenate([low, none], axis=0), 1, 1)
+                + dd(pick2, jnp.concatenate([none, high], axis=0), 1, 1)
+                + dd(pick2, jnp.concatenate([none, low], axis=0), 1, 1)
+            )
+        ref["s"][n, pl.ds(c, 1), span, :] = chosen[None]
+        spread(*s_at(n, g))
+
+    done = set()
+
+    def finish(s):
+        k, g = stages[s]
+        start, stop = groups[g]
+        for index in (3, 4, 5, 6):
+            live[s, index].wait_recv()
+        fin = ref[f"f{s}"]
+        out = ref[f"t{s}"]
+        for base, one, two in ((0, 0, 3), (half, 1, 2)):
+
+            def body(i, base=base, one=one, two=two):
+                at = pl.ds(pl.multiple_of(i + base, 8), 8)
+                out[0, at, :] = out[0, at, :] + (fin[one, pl.ds(i, 8), :] + fin[two, pl.ds(i, 8), :])
+
+            strips(half, body)
+        count = (stop - start) * width
+        span = slice(start * width, stop * width)
+        high, low = halves_of(out[0, :, :count])
+        ref["y_h"][k * height : (k + 1) * height, span] = high
+        ref["y_l"][k * height : (k + 1) * height, span] = low
+        into, at, target = ("o_one", k, "out_one") if k < first else ("o_two", 0, "out_two")
+        for j in range(start, stop):
+            ref[into][at, j] = -out[0, :, (j - start) * width : (j + 1 - start) * width]
+        write(ref[into].at[at, start:stop], ref[target].at[at, start:stop])
+        done.add(s)
+        if k >= first:
+            choose(1, g)
+            return (1, g)
+        if all(names_of[other, g] in done for other in range(first)):
+            choose(0, g)
+            return (0, g)
+        return None
+
+    def order_one(q):
+        take = ones_at(iota((col_pad, entries), 0) == jnp.where(c_owner1 == q, c_slot1, -1))
+        ref["c1_h"][q] = dd(take, ref["ph"][:, :fringe]).astype(BF16)
+        ref["c1_l"][q] = dd(take, ref["pl"][:, :fringe]).astype(BF16)
+
+    def order_two(q):
+        mark = jnp.where((c_owner2 == q) & above, c_slot2, -1)
+        place = (over(row2, TILE) - tiles) * width + within(row2, width)
+        mark = jnp.where((c_owner2 == q) & (row2 >= tiles * TILE), col_pad + place, mark)
+        take = ones_at(iota((col_pad + fringe, entries), 0) == mark)
+        high = dd(take, ref["ph"][:, fringe:]).astype(BF16)
+        low = dd(take, ref["pl"][:, fringe:]).astype(BF16)
+        ref["c2_h"][q] = high[:col_pad]
+        ref["c2_l"][q] = low[:col_pad]
+        ref["cl_h"][q] = high[col_pad:]
+        ref["cl_l"][q] = low[col_pad:]
+
+    aside = [lambda: forward(*v_at(first))]
+    aside += [lambda q=q: order_one(q) for q in range(cols)]
+    aside += [lambda q=q: order_two(q) for q in range(cols)]
+    pending = []
+    begun = set()
+
+    def settle(s, now):
+        if s not in done:
+            piece = finish(s)
+            if piece is not None:
+                pending.append((now + 2, piece))
+
+    for step in range(len(stages) + 3):
+        if step >= 3:
+            settle(step - 3, step)
+        if step < len(stages):
+            k, g = stages[step]
+            if k not in begun:
+                begun.add(k)
+                ready(k)
+            if k >= first:
+                for other in range(first):
+                    settle(names_of[other, g], step)
+            begin(step)
+        if aside:
+            aside.pop(0)()
+        if step < len(stages):
+            push(step)
+        if 2 <= step < len(stages) + 2:
+            middle(step - 2)
+        while pending and pending[0][0] <= step:
+            forward(*s_at(*pending.pop(0)[1]))
+    for work in aside:
+        work()
+    for _, piece in pending:
+        forward(*s_at(*piece))
+
+    def turned(n, q):
+        return halves_of(grown(ref["s"][n, q], col_pad).T)
+
+    for g in range(len(groups)):
+        arrive(*s_at(0, g))
+    corner = jnp.zeros((edge, fringe), F32)
+    for q in range(cols):
+        corner = corner + three(turned(0, q), (ref["c1_h"][q], ref["c1_l"][q]))
+    for k in range(first):
+        for kk in range(first):
+            piece = corner[k * height : (k + 1) * height, kk * width : (kk + 1) * width]
+            ref["o_one"][k, tiles + kk] = ref["d_one"][k, kk] + piece
+        write(ref["o_one"].at[k, tiles:], ref["out_one"].at[k, tiles:])
+    for g in range(len(groups)):
+        arrive(*s_at(1, g))
+    cross = jnp.zeros((2 * height, fringe), F32)
+    final = jnp.zeros((2 * height, width), F32)
+    for q in range(cols):
+        both = turned(1, q)
+        cross = cross + three(both, (ref["c1_h"][q], ref["c1_l"][q]))
+        final = final + three(both, (ref["c2_h"][q], ref["c2_l"][q]))
+    tail = ref[f"t{len(stages) - 1}"]
+    bottom = cross[:height] - tail[0, :, tail.shape[2] - fringe :]
+    ref["b"][pl.ds(c, 1)] = bottom[None]
+    for step in range(1, cols):
+        other = (c + step) % cols
+        launch(
+            remote(
+                ref["b"].at[c], ref["b"].at[c], ref["b_send"].at[step], ref["b_recv"].at[c], r, other
+            )
+        )
+    for kk in range(first):
+        ref["o_two"][0, tiles + kk] = bottom[:, kk * width : (kk + 1) * width]
+    for step in range(1, cols):
+        other = (c + step) % cols
+        remote(
+            ref["b"].at[other], ref["b"].at[other], ref["b_send"].at[step], ref["b_recv"].at[other], r, other
+        ).wait_recv()
+    result = ref["d_two"][0, 0] + final[height:]
+    for q in range(cols):
+        result = result - three(halves_of(ref["b"][q]), (ref["cl_h"][q], ref["cl_l"][q]))
+    ref["o_two"][0, tiles + first] = result
+    write(ref["o_two"].at[0, tiles:], ref["out_two"].at[0, tiles:])
+
+    for copy in sent:
+        copy.wait_send()
+    for go, copy in drains:
+
+        @pl.when(go)
+        def _(copy=copy):
+            copy().wait_send()
+
+    for copy in writes:
+        copy.wait()
+
+
+def on_device_fused(
+    ancestor,
+    inverse_first,
+    panel_first,
+    structure_first,
+    inverse_second,
+    panel_second,
+    structure_second,
+):
+    rows = lax.axis_size("row")
+    cols = lax.axis_size("col")
+    height = TILE // rows
+    width = TILE // cols
+    tiles = ancestor.shape[0]
+    first = inverse_first.shape[0]
+    entries = structure_first.shape[0]
+    chunks = first + 1
+    wide = tiles * width
+    row_slots = tiles * height // GRAIN * CAP
+    low_slots = first * height // GRAIN * CAP
+    col_slots = wide // GRAIN * CAP
+    row_pad = -(-row_slots // 128) * 128
+    col_pad = -(-col_slots // 128) * 128
+    edge = first * height
+    fringe = first * width
+    parts = min(3, tiles)
+    groups = [(i * tiles // parts, (i + 1) * tiles // parts) for i in range(parts)]
+    widest = max(stop - start for start, stop in groups) * width
+    stages = chunks * parts
+    dma = pltpu.SemaphoreType.DMA
+    scratch = {
+        "a": pltpu.VMEM((tiles, tiles, height, width), F32),
+        "d_one": pltpu.VMEM((first, first, height, width), F32),
+        "d_two": pltpu.VMEM((1, 1, height, width), F32),
+        "o_one": pltpu.VMEM((first, tiles + first, height, width), F32),
+        "o_two": pltpu.VMEM((1, tiles + first + 1, height, width), F32),
+        "pall": pltpu.VMEM((chunks, entries, width), F32),
+        "ph": pltpu.VMEM((entries, chunks * width), BF16),
+        "pl": pltpu.VMEM((entries, chunks * width), BF16),
+        "kept_h": pltpu.VMEM((2, row_pad, wide), BF16),
+        "kept_l": pltpu.VMEM((2, row_pad, wide), BF16),
+        "v_one": pltpu.VMEM((first, cols, row_slots, width), F32),
+        "v_two": pltpu.VMEM((cols, row_slots + low_slots, width), F32),
+        "turned": pltpu.VMEM((chunks, 8 * width, row_pad), BF16),
+        "under": pltpu.VMEM((8 * width, edge), BF16),
+        "y_h": pltpu.VMEM((chunks * height, wide), BF16),
+        "y_l": pltpu.VMEM((chunks * height, wide), BF16),
+        "d_h": pltpu.VMEM((edge, fringe), BF16),
+        "d_l": pltpu.VMEM((edge, fringe), BF16),
+        "pick": pltpu.VMEM((2, col_slots, widest), BF16),
+        "s": pltpu.VMEM((2, cols, col_slots, 2 * height), F32),
+        "c1_h": pltpu.VMEM((cols, col_pad, fringe), BF16),
+        "c1_l": pltpu.VMEM((cols, col_pad, fringe), BF16),
+        "c2_h": pltpu.VMEM((cols, col_pad, width), BF16),
+        "c2_l": pltpu.VMEM((cols, col_pad, width), BF16),
+        "cl_h": pltpu.VMEM((cols, fringe, width), BF16),
+        "cl_l": pltpu.VMEM((cols, fringe, width), BF16),
+        "b": pltpu.VMEM((cols, height, fringe), F32),
+        "l_sem": dma((3,)),
+        "w_sem": dma((stages + first + 1,)),
+        "g_send": dma((chunks, 7)),
+        "g_recv": dma((chunks, 7)),
+        "v_send": dma((chunks, 6)),
+        "v_recv": dma((chunks, cols)),
+        "r_send": dma((stages, 7)),
+        "r_recv": dma((stages, 7)),
+        "s_send": dma((2, parts, 6)),
+        "s_recv": dma((2, parts, cols)),
+        "b_send": dma((cols,)),
+        "b_recv": dma((cols,)),
+    }
+    for s in range(stages):
+        k, g = (first, s - first * parts) if s >= first * parts else (s % first, s // first)
+        size = (groups[g][1] - groups[g][0]) * width
+        if s == stages - 1:
+            size += fringe
+        scratch[f"z{s}"] = pltpu.VMEM((2, 4, height, size), F32)
+        scratch[f"m{s}"] = pltpu.VMEM((4, height, size), F32)
+        scratch[f"t{s}"] = pltpu.VMEM((4, height, size), F32)
+        scratch[f"i{s}"] = pltpu.VMEM((2, height // 2, size), F32)
+        scratch[f"f{s}"] = pltpu.VMEM((4, height // 2, size), F32)
+    inputs = ["ancestor", "diag_one", "diag_two", "panel_one", "panel_two", "list_one", "list_two"]
+    names = inputs + ["out_one", "out_two"] + list(scratch)
+    vmem = pl.BlockSpec(memory_space=pltpu.VMEM)
+    hbm = pl.BlockSpec(memory_space=pl.ANY)
+    dims = (rows, cols, height, width, tiles, first, entries, groups)
+    return pl.pallas_call(
+        functools.partial(fused, dims, names),
+        out_shape=(
+            jax.ShapeDtypeStruct((first, tiles + first, height, width), F32),
+            jax.ShapeDtypeStruct((1, tiles + first + 1, height, width), F32),
+        ),
+        in_specs=[hbm] * 3 + [vmem] * 4,
+        out_specs=(hbm, hbm),
+        scratch_shapes=list(scratch.values()),
+        compiler_params=pltpu.CompilerParams(
+            collective_id=0, has_side_effects=True, vmem_limit_bytes=60 * 1024 * 1024
+        ),
+    )(
+        open_packed(ancestor, height, width),
+        open_packed(inverse_first, height, width),
+        open_packed(inverse_second, height, width),
+        panel_first.transpose(1, 0, 2),
+        panel_second.transpose(1, 0, 2),
+        structure_first,
+        structure_second,
+    )
+
+
+def fits(rows, cols):
+    return rows == 8 and rows == 2 * cols and TILE // cols % 128 == 0
+
 
 def solution(mesh):
+    body = on_device_fused if fits(mesh.shape["row"], mesh.shape["col"]) else on_device
     in_specs = (
         P(None, None, "row", "col"),
         P(None, None, "row", "col"),
@@ -225,5 +921,5 @@
     )
     out_specs = (P(None, None, "row", "col"), P(None, None, "row", "col"))
     return jax.shard_map(
-        on_device, mesh=mesh, in_specs=in_specs, out_specs=out_specs, check_vma=False
-    )
+        body, mesh=mesh, in_specs=in_specs, out_specs=out_specs, check_vma=False
+    )

time: 280 us -> 127 us (0.45); the launches traced: 275 us -> 127 us
  waiting for transfers between devices: 164 us -> 0 us
  Pallas kernels: 0 us -> 121 us
  matrix products: 35.5 us -> 0 us
  local copies, waits for them, and re-layouts: 27.7 us -> 5.43 us
  other arithmetic: 18.6 us -> 0 us
  blocking collectives: 14.1 us -> 0 us
  between operations: 14.5 us -> 0.64 us
    pallas_call x0 -> x1, Pallas kernels: none -> 121 us  [on_device_fused(): pl.pallas_call(functools.partial(fused, dims, names), out_shape=(jax.Shap...]
    all_gather x3 -> x0, waiting for transfers between devices: 96.3 us -> none  [the longest x1 39.3 us: on_device(): lax.all_gather(jnp.concatenate([part_first, part_second], axis=0), 'col',...]
    reduce_scatter x1 -> x0, waiting for transfers between devices: 67.3 us -> none  [on_device(): summed = lax.psum_scatter(joined, 'row', scatter_dimension=0, tiled=False)]
    dot_general x16 -> x0, matrix products: 35.5 us -> none  [product(): lax.dot_general(left, right, (((left_dim,), (0,)), ((), ())), precision=l...]
    all_gather x1 -> x0, blocking collectives: 14.1 us -> none  [on_device(): low_all = lax.all_gather(low_block, 'col', axis=0)]
    slice x11 -> x0, local copies, waits for them, and re-layouts: 9.2 us -> none  [the longest x1 2.4 us: on_device(): spread[:, cut:].reshape(cols, row_slots + low_slots, halves, second, height)]
    concatenate x7 -> x0, other arithmetic: 7.48 us -> none  [the longest x1 3.89 us: on_device(): joined = jnp.concatenate([partial, jnp.concatenate(slabs, axis=1)], axis=2)]
    reduce_sum x2 -> x0, other arithmetic: 5.33 us -> none  [entry_ranks(): return jnp.sum(same.astype(jnp.int32), axis=1)]
  transfers between devices with their start and end apart: 4 -> 0, of which waited for: 4 -> 0; matrix products, arithmetic and copies ran while one was open for 10% -> 0% of each run, Pallas kernels for 0% -> 0%
where the time goes in v2:
time: 127 us
  Pallas kernels  121 us (95%)
  local copies, waits for them, and re-layouts  5.43 us (4%)
    pallas_call x1, Pallas kernels, on_device_fused(): pl.pallas_call(functools.partial(fused, dims, names), out_shape=(jax.Shap...  121 us
    unnamed x3, local copies, waits for them, and re-layouts  5.43 us

profile of v2, /device:TPU:0, one launch (start us, length us, event | category | flops | bytes accessed | tf_op | source)
XLA Modules:
  0.0 126.6 jit_solution(10635081687045930597)
XLA Ops:
  0.6 1.6 %copy.11 = f32[192,2,128]{2,0,1:T(8,128)} copy(f32[192,2,128]{2,1,0:T(2,128)} %param.9) | data formatting | bytes 393216 | tf_op args[2]
  2.2 120.5 %shard_map.86 = (f32[2,11,64,128]{3,2,1,0:T(8,128)}, f32[1,12,64,128]{3,2,1,0:T(8,128)}) custom-call(f32[9,9,64,128]{3,2,1,0:T(8,128)} %refs_0_.1, f32[2,2,64,128]{3,2,1,0:T(8,128)} %refs_1_.1, f32[1,1,64,128]{3,2,1,0:T(8,128)} %refs_2_.1, f32[2,192,128]{2,1,0:T(8,128)} %bitcast.4, f32[1,192,128]{2,1,0:T(8,128)} %bitcast.5, s32[1536]{0:T(1024)} %refs_5_.1, ...), custom_call_target="tpu_custom_call" | custom-call | tf_op jit(solution)/shard_map/pallas_call | solution.py:884
  122.8 2.0 %copy.14 = f32[2,11,64,128]{3,2,1,0:T(8,128)} copy(f32[2,11,64,128]{3,2,1,0:T(8,128)} %get-tuple-element.4) | data formatting | bytes 1441792
  124.8 1.8 %copy.15 = f32[1,12,64,128]{3,2,1,0:T(8,128)} copy(f32[1,12,64,128]{3,2,1,0:T(8,128)} %get-tuple-element.5) | data formatting | bytes 786432

commit v3 on v2

--- a/solution.py
+++ b/solution.py
@@ -254,11 +254,17 @@
 
 def grown(value, count):
     rest = count - value.shape[0]
+    if not rest:
+        return value
     return jnp.concatenate([value, jnp.zeros((rest, value.shape[1]), value.dtype)], axis=0)
 
 
 def spots(hits, places):
     return jnp.max(jnp.where(hits, places, -1.0), axis=1, keepdims=True)
+
+
+def order_of(first, parts):
+    return [(k, g) for k in range(first + 1) for g in range(parts)]
 
 
 def fused(dims, names, *refs):
@@ -275,7 +281,6 @@
     edge = first * height
     fringe = first * width
     row_pad = -(-row_slots // 128) * 128
-    col_pad = -(-col_slots // 128) * 128
     half = height // 2
 
     r = lax.axis_index("row")
@@ -295,8 +300,7 @@
         y = 1 - chip_y if rel // 2 else chip_y
         return y * 2 + x
 
-    sent = []
-    drains = []
+    ends = []
 
     def remote(source, target, send, recv, device, column=None):
         return pltpu.make_async_remote_copy(
@@ -310,8 +314,10 @@
 
     def launch(copy):
         copy.start()
-        sent.append(copy)
         return copy
+
+    def sent(whole, sem, go=None):
+        ends.append((go, lambda: remote(whole(), whole(), sem, sem, mate).wait_send()))
 
     barrier = pltpu.get_barrier_semaphore()
     for peer in (mate, by_x, by_y, by_both):
@@ -319,12 +325,20 @@
     for step in range(1, cols):
         other = (c + step) % cols
         pl.semaphore_signal(barrier, inc=1, device_id=(r, other), device_id_type=MESH)
-    loads = []
-    for index, (source, target) in enumerate(
-        (("ancestor", "a"), ("diag_one", "d_one"), ("diag_two", "d_two"))
-    ):
-        loads.append(pltpu.make_async_copy(ref[source], ref[target], ref["l_sem"].at[index]))
-        loads[-1].start()
+    loads = {}
+
+    def load(name, source, target):
+        loads[name] = pltpu.make_async_copy(source, target, ref["l_sem"].at[len(loads)])
+        loads[name].start()
+
+    load("list_one", ref["list_one"], ref["l_one"])
+    load("list_two", ref["list_two"], ref["l_two"])
+    for k in range(chunks):
+        source = ref["panel_one"].at[:, k] if k < first else ref["panel_two"].at[:, k - first]
+        load(k, source, ref["own"].at[k])
+    load("a", ref["ancestor"], ref["a"])
+    load("d_one", ref["diag_one"], ref["d_one"])
+    load("d_two", ref["diag_two"], ref["d_two"])
 
     def ranks(row):
         group = over(row, GRAIN)
@@ -347,8 +361,10 @@
         place = over(row, TILE) * size + within(row, size)
         return owner, group * CAP + rank, place.astype(F32)
 
-    row1 = ref["list_one"][...].reshape(1, entries)
-    row2 = ref["list_two"][...].reshape(1, entries)
+    loads["list_one"].wait()
+    loads["list_two"].wait()
+    row1 = ref["l_one"][...].reshape(1, entries)
+    row2 = ref["l_two"][...].reshape(1, entries)
     rank1 = ranks(row1)
     rank2 = ranks(row2)
     above = row2 < tiles * TILE
@@ -367,23 +383,22 @@
     def own_rows(device):
         return pl.ds(pl.multiple_of(device * shard, 8), shard)
 
-    def panel(k):
-        return ref["panel_one"].at[k] if k < first else ref["panel_two"].at[k - first]
-
     gather = {}
     for k in range(chunks):
+        loads[k].wait()
         for rel, peer in (*peers.items(), (0, mate)):
             gather[k, rel] = launch(
                 remote(
-                    panel(k),
+                    ref["own"].at[k],
                     pall.at[k, own_rows(r)],
-                    ref["g_send"].at[k, rel],
+                    ref["g_send"].at[k],
                     ref["g_recv"].at[k, rel],
                     peer,
                 )
             )
+        sent(lambda k=k: pall.at[k, pl.ds(0, 7 * shard)], ref["g_send"].at[k])
     for k in range(chunks):
-        pall[k, own_rows(r), :] = panel(k)[...]
+        pall[k, own_rows(r), :] = ref["own"][k]
 
     def keep(at, marks, places):
         spot = spots(iota((row_pad, entries), 0) == marks, places)
@@ -399,68 +414,66 @@
 
         lax.fori_loop(0, tiles, step, 0)
 
-    def spread(at, sends, recvs):
-        for index, (sign, reach) in enumerate(((1, 2), (-1, 2), (1, 1), (-1, 1))):
+    def spread(at, sends, recvs, whole, direct=False):
+        for sign, reach in ((1, 3), (-1, 3), (1, 2), (-1, 2), (1, 1), (-1, 1)):
             there = c + sign * reach
-            go = (there >= 0) & (there < cols)
-
-            def copy(there=there, index=index):
-                return remote(at(c), at(c), sends.at[index], recvs.at[c], r, there)
-
-            @pl.when(go)
-            def _(copy=copy):
-                copy().start()
-
-            drains.append((go, copy))
-
-    def forward(at, sends, recvs):
-        for index, sign in ((4, 1), (5, -1)):
+            if reach < cols - 1 or direct:
+
+                @pl.when((there >= 0) & (there < cols))
+                def _(there=there):
+                    remote(at(c), at(c), sends, recvs.at[c], r, there).start()
+
+        if direct:
+            sent(lambda: whole(cols - 1), sends)
+        else:
+            edge_of = (c == 0) | (c == cols - 1)
+            sent(lambda: whole(2), sends, edge_of)
+            sent(lambda: whole(4), sends, jnp.logical_not(edge_of))
+
+    def forward(at, sends, recvs, whole, direct=False):
+        if direct:
+            return
+        for sign in (1, -1):
             q = c - 2 * sign
             there = c + sign
-            go = (q >= 0) & (q < cols) & (there >= 0) & (there < cols)
-
-            def copy(q=q, there=there, index=index):
-                return remote(at(q), at(q), sends.at[index], recvs.at[q], r, there)
-
-            @pl.when(go)
-            def _(copy=copy):
-                copy().wait_recv()
-                copy().start()
-
-            drains.append((go, copy))
-
-    def arrive(at, sends, recvs):
+
+            @pl.when((q >= 0) & (q < cols) & (there >= 0) & (there < cols))
+            def _(q=q, there=there):
+                copy = remote(at(q), at(q), sends, recvs.at[q], r, there)
+                copy.wait_recv()
+                copy.start()
+
+    def arrive(at, sends, recvs, whole, direct=False):
         for reach in range(1, cols):
             for sign in (1, -1):
                 q = c - reach * sign
                 there = c + sign
                 go = (q >= 0) & (q < cols)
-                if reach == 2:
+                if reach == 2 and not direct:
                     go = go & ((there < 0) | (there >= cols))
 
                 @pl.when(go)
                 def _(q=q):
-                    remote(at(q), at(q), sends.at[0], recvs.at[q], r, c).wait_recv()
+                    remote(at(q), at(q), sends, recvs.at[q], r, c).wait_recv()
 
     def v_at(k):
-        if k < first:
-            return (lambda q: ref["v_one"].at[k, q]), ref["v_send"].at[k], ref["v_recv"].at[k]
-        return (lambda q: ref["v_two"].at[q]), ref["v_send"].at[k], ref["v_recv"].at[k]
+        buf = ref["v_one"].at[k] if k < first else ref["v_two"]
+        return buf.at.__getitem__, ref["v_send"].at[k], ref["v_recv"].at[k], lambda n: buf.at[pl.ds(0, n)]
 
     one_rows = -(-row_slots // 16) * 16
     two_rows = -(-(row_slots + low_slots) // 16) * 16
     take1 = ones_at(iota((one_rows, entries), 0) == mark1)
-    loads[0].wait()
+    loads["a"].wait()
     keep(0, mark1, r_place1)
     for k in range(chunks):
         for rel in (1, 2, 3):
             gather[k, rel].wait_recv()
             part = pall.at[k, own_rows(peers[rel])]
             gather[k, 3 + rel] = launch(
-                remote(part, part, ref["g_send"].at[k, 3 + rel], ref["g_recv"].at[k, 3 + rel], mate)
+                remote(part, part, ref["g_send"].at[k], ref["g_recv"].at[k, 0], mate)
             )
-        for rel in (0, 4, 5, 6):
-            gather[k, rel].wait_recv()
+        four = pall.at[k, pl.ds(0, 4 * shard)]
+        remote(four, four, ref["g_send"].at[k], ref["g_recv"].at[k, 0], mate).wait_recv()
         high, low = halves_of(pall[k])
         span = slice(k * width, (k + 1) * width)
         ref["ph"][:, span] = high
@@ -478,8 +491,8 @@
     keep(1, upper2, r_place2)
     low_spot = spots(iota((128, entries), 0) == lower2, r_place2 - float(tall))
     spread_low = ones_at(low_spot == iota((128, edge), 1).astype(F32))
-    for load in loads[1:]:
-        load.wait()
+    loads["d_one"].wait()
+    loads["d_two"].wait()
     for k in range(first):
         for kk in range(first):
             high, low = halves_of(ref["d_one"][k, kk])
@@ -524,8 +537,7 @@
         both = dd(left, high)
         return both[:count] + both[count:] + dd(left[:count], low)
 
-    stages = [(k, g) for g in range(len(groups)) for k in range(first)]
-    stages += [(first, g) for g in range(len(groups))]
+    stages = order_of(first, len(groups))
     names_of = {stage: s for s, stage in enumerate(stages)}
     live = {}
 
@@ -533,7 +545,7 @@
         for rel in range(4):
             for side in range(2):
                 top = rel * width + side * height
-                ref[f"z{s}"][side, rel, :, start:stop] = part[top : top + height]
+                ref[f"z{s}"][side * 4 + rel, :, start:stop] = part[top : top + height]
 
     def begin(s):
         k, g = stages[s]
@@ -550,13 +562,14 @@
             put(s, part, count, count + fringe)
         live[s, 0] = launch(
             remote(
-                ref[f"z{s}"].at[1 - core],
+                ref[f"z{s}"].at[pl.ds((1 - core) * 4, 4)],
                 ref[f"m{s}"],
-                ref["r_send"].at[s, 0],
+                ref["r_send"].at[s],
                 ref["r_recv"].at[s, 0],
                 mate,
             )
         )
+        sent(lambda: ref[f"z{s}"].at[pl.ds(0, 7)], ref["r_send"].at[s])
 
     def strips(count, body):
         def step(i, carry):
@@ -567,7 +580,7 @@
 
     def pass_on(s, index, source, target, peer):
         live[s, index] = launch(
-            remote(source, target, ref["r_send"].at[s, index], ref["r_recv"].at[s, index], peer)
+            remote(source, target, ref["r_send"].at[s], ref["r_recv"].at[s, min(index, 3)], peer)
         )
 
     lower = pl.ds(0, half)
@@ -583,7 +596,7 @@
         def pair(rel):
             def body(i):
                 at = pl.ds(i, 8)
-                mine = own[pl.ds(core, 1), rel, at, :].reshape(8, count)
+                mine = own[pl.ds(core * 4 + rel, 1), at, :].reshape(8, count)
                 total[rel, at, :] = mine + got[rel, at, :]
 
             strips(height, body)
@@ -623,32 +636,37 @@
         copy.start()
         writes.append(copy)
 
+    def counted(g):
+        start, stop = groups[g]
+        count = (stop - start) * tile_slots // 2
+        return count, -(-count * cols // 128) * 128
+
     def s_at(n, g):
-        start, stop = groups[g]
-        span = pl.ds(start * tile_slots, (stop - start) * tile_slots)
-        return (lambda q: ref["s"].at[n, q, span]), ref["s_send"].at[n, g], ref["s_recv"].at[n, g]
+        buf = ref[f"s{n}{g}"]
+        direct = n >= first and g == len(groups) - 1
+        sems = ref["s_send"].at[n, g], ref["s_recv"].at[n, g]
+        return buf.at.__getitem__, *sems, lambda k: buf.at[pl.ds(0, k)], direct
 
     def choose(n, g):
         start, stop = groups[g]
-        span = slice(start * tile_slots, stop * tile_slots)
+        top = start * tile_slots
+        half_count = counted(g)[0]
         count = (stop - start) * width
         columns = slice(start * width, stop * width)
-        pick1 = ref["pick"][0, span, :count]
-        if n == 0:
-            chosen = dd(pick1, ref["y_h"][:edge, columns], 1, 1)
-            chosen = chosen + dd(pick1, ref["y_l"][:edge, columns], 1, 1)
-        else:
-            pick2 = ref["pick"][1, span, :count]
-            high = ref["y_h"][edge:, columns]
-            low = ref["y_l"][edge:, columns]
-            none = jnp.zeros_like(high)
-            chosen = (
-                dd(pick1, jnp.concatenate([high, none], axis=0), 1, 1)
-                + dd(pick1, jnp.concatenate([low, none], axis=0), 1, 1)
-                + dd(pick2, jnp.concatenate([none, high], axis=0), 1, 1)
-                + dd(pick2, jnp.concatenate([none, low], axis=0), 1, 1)
-            )
-        ref["s"][n, pl.ds(c, 1), span, :] = chosen[None]
+        which = n // chunks
+        chunk = min(n, first) * height
+        near = ref["pick"][which, top : top + half_count, :count]
+        far = ref["pick"][which, top + half_count : top + 2 * half_count, :count]
+        high = ref["y_h"][chunk : chunk + height, columns]
+        low = ref["y_l"][chunk : chunk + height, columns]
+        none = jnp.zeros_like(high)
+        chosen = (
+            dd(near, jnp.concatenate([high, none], axis=0), 1, 1)
+            + dd(near, jnp.concatenate([low, none], axis=0), 1, 1)
+            + dd(far, jnp.concatenate([none, high], axis=0), 1, 1)
+            + dd(far, jnp.concatenate([none, low], axis=0), 1, 1)
+        )
+        ref[f"s{n}{g}"][pl.ds(c, 1)] = chosen[None]
         spread(*s_at(n, g))
 
     done = set()
@@ -656,9 +674,8 @@
     def finish(s):
         k, g = stages[s]
         start, stop = groups[g]
-        for index in (3, 4, 5, 6):
-            live[s, index].wait_recv()
         fin = ref[f"f{s}"]
+        remote(fin, fin, ref["r_send"].at[s], ref["r_recv"].at[s, 3], mate).wait_recv()
         out = ref[f"t{s}"]
         for base, one, two in ((0, 0, 3), (half, 1, 2)):
 
@@ -677,122 +694,168 @@
             ref[into][at, j] = -out[0, :, (j - start) * width : (j + 1 - start) * width]
         write(ref[into].at[at, start:stop], ref[target].at[at, start:stop])
         done.add(s)
-        if k >= first:
-            choose(1, g)
-            return (1, g)
-        if all(names_of[other, g] in done for other in range(first)):
-            choose(0, g)
-            return (0, g)
-        return None
-
-    def order_one(q):
-        take = ones_at(iota((col_pad, entries), 0) == jnp.where(c_owner1 == q, c_slot1, -1))
-        ref["c1_h"][q] = dd(take, ref["ph"][:, :fringe]).astype(BF16)
-        ref["c1_l"][q] = dd(take, ref["pl"][:, :fringe]).astype(BF16)
-
-    def order_two(q):
-        mark = jnp.where((c_owner2 == q) & above, c_slot2, -1)
+        choose(k, g)
+
+    def order(at, owner, slot, g, keep_if):
+        start, stop = groups[g]
+        half_count, region = counted(g)
+        inside = slot - start * tile_slots
+        side = (inside >= half_count).astype(jnp.int32)
+        mark = side * region + owner * half_count + inside - side * half_count
+        mark = jnp.where((inside >= 0) & (inside < 2 * half_count) & keep_if, mark, -1)
+        take = ones_at(iota((2 * region, entries), 0) == mark)
+        span = slice(0, fringe) if at == 1 else slice(fringe, fringe + width)
+        for part, name in (("ph", "h"), ("pl", "l")):
+            ref[f"c{at}{g}{name}"][...] = dd(take, ref[part][:, span]).astype(BF16)
+
+    def order_one(g):
+        order(1, c_owner1, c_slot1, g, c_owner1 >= 0)
+
+    def order_two(g):
+        order(2, c_owner2, c_slot2, g, above)
+
+    def order_low():
         place = (over(row2, TILE) - tiles) * width + within(row2, width)
-        mark = jnp.where((c_owner2 == q) & (row2 >= tiles * TILE), col_pad + place, mark)
-        take = ones_at(iota((col_pad + fringe, entries), 0) == mark)
-        high = dd(take, ref["ph"][:, fringe:]).astype(BF16)
-        low = dd(take, ref["pl"][:, fringe:]).astype(BF16)
-        ref["c2_h"][q] = high[:col_pad]
-        ref["c2_l"][q] = low[:col_pad]
-        ref["cl_h"][q] = high[col_pad:]
-        ref["cl_l"][q] = low[col_pad:]
-
-    aside = [lambda: forward(*v_at(first))]
-    aside += [lambda q=q: order_one(q) for q in range(cols)]
-    aside += [lambda q=q: order_two(q) for q in range(cols)]
+        mark = jnp.where(above, -1, c_owner2 * fringe + place)
+        take = ones_at(iota((cols * fringe, entries), 0) == mark)
+        ref["cl_h"][...] = dd(take, ref["ph"][:, fringe:]).astype(BF16)
+        ref["cl_l"][...] = dd(take, ref["pl"][:, fringe:]).astype(BF16)
+
+    asides = {0: [lambda: forward(*v_at(first))]}
+    for index, work in enumerate(
+        [lambda g=g: order_one(g) for g in range(len(groups))]
+        + [lambda g=g: order_two(g) for g in range(len(groups))]
+        + [order_low]
+    ):
+        asides.setdefault(1 + index // 2, []).append(work)
     pending = []
     begun = set()
 
     def settle(s, now):
         if s not in done:
-            piece = finish(s)
-            if piece is not None:
-                pending.append((now + 2, piece))
-
-    for step in range(len(stages) + 3):
-        if step >= 3:
-            settle(step - 3, step)
-        if step < len(stages):
-            k, g = stages[step]
-            if k not in begun:
-                begun.add(k)
-                ready(k)
-            if k >= first:
-                for other in range(first):
-                    settle(names_of[other, g], step)
-            begin(step)
-        if aside:
-            aside.pop(0)()
-        if step < len(stages):
-            push(step)
-        if 2 <= step < len(stages) + 2:
+            finish(s)
+            pending.append((now + 2, stages[s]))
+
+    def relay(now):
+        while pending and pending[0][0] <= now:
+            forward(*s_at(*pending.pop(0)[1]))
+
+    gap = 4
+    count = len(stages)
+    for step in range(count):
+        if step >= gap:
+            settle(step - gap, step)
+        k, g = stages[step]
+        if k not in begun:
+            begun.add(k)
+            ready(k)
+        if k >= first:
+            for other in range(first):
+                settle(names_of[other, g], step)
+        begin(step)
+        for work in asides.pop(step, []):
+            work()
+        if step >= 2:
             middle(step - 2)
-        while pending and pending[0][0] <= step:
-            forward(*s_at(*pending.pop(0)[1]))
-    for work in aside:
-        work()
-    for _, piece in pending:
-        forward(*s_at(*piece))
-
-    def turned(n, q):
-        return halves_of(grown(ref["s"][n, q], col_pad).T)
-
+        push(step)
+        relay(step)
+    for works in asides.values():
+        for work in works:
+            work()
+    middle(count - 2)
+    relay(count)
+
+    def own_rows_of(g):
+        choose(chunks, g)
+        pending.append((count + 2, (chunks, g)))
+
+    for index in range(len(groups)):
+        settle(count - len(groups) + index, count)
+        own_rows_of(index)
+        if index == 0:
+            middle(count - 1)
+        else:
+            relay(count + 2)
+    relay(count + 2)
+
+    def side_by_side(n, g):
+        region = counted(g)[1]
+        buf = ref[f"s{n}{g}"]
+        return halves_of(grown(jnp.concatenate([buf[q] for q in range(cols)], axis=0), region).T)
+
+    def ordered(at, g, side):
+        region = counted(g)[1]
+        span = slice(side * region, (side + 1) * region)
+        return ref[f"c{at}{g}h"][span], ref[f"c{at}{g}l"][span]
+
+    def crossed(n, g, at):
+        arrive(*s_at(n, g))
+        both = side_by_side(n, g)
+        near = three(both, ordered(at, g, 0))[:height]
+        return near + three(both, ordered(at, g, 1))[height:]
+
+    cross = jnp.zeros((height, fringe), F32)
     for g in range(len(groups)):
-        arrive(*s_at(0, g))
-    corner = jnp.zeros((edge, fringe), F32)
-    for q in range(cols):
-        corner = corner + three(turned(0, q), (ref["c1_h"][q], ref["c1_l"][q]))
-    for k in range(first):
-        for kk in range(first):
-            piece = corner[k * height : (k + 1) * height, kk * width : (kk + 1) * width]
-            ref["o_one"][k, tiles + kk] = ref["d_one"][k, kk] + piece
-        write(ref["o_one"].at[k, tiles:], ref["out_one"].at[k, tiles:])
-    for g in range(len(groups)):
-        arrive(*s_at(1, g))
-    cross = jnp.zeros((2 * height, fringe), F32)
-    final = jnp.zeros((2 * height, width), F32)
-    for q in range(cols):
-        both = turned(1, q)
-        cross = cross + three(both, (ref["c1_h"][q], ref["c1_l"][q]))
-        final = final + three(both, (ref["c2_h"][q], ref["c2_l"][q]))
+        cross = cross + crossed(first, g, 1)
     tail = ref[f"t{len(stages) - 1}"]
-    bottom = cross[:height] - tail[0, :, tail.shape[2] - fringe :]
+    bottom = cross - tail[0, :, tail.shape[2] - fringe :]
     ref["b"][pl.ds(c, 1)] = bottom[None]
     for step in range(1, cols):
         other = (c + step) % cols
         launch(
             remote(
-                ref["b"].at[c], ref["b"].at[c], ref["b_send"].at[step], ref["b_recv"].at[c], r, other
+                ref["b"].at[c], ref["b"].at[c], ref["b_send"], ref["b_recv"].at[c], r, other
             )
         )
+    sent(lambda: ref["b"].at[pl.ds(0, cols - 1)], ref["b_send"])
     for kk in range(first):
         ref["o_two"][0, tiles + kk] = bottom[:, kk * width : (kk + 1) * width]
+    for k in range(first):
+        corner = jnp.zeros((height, fringe), F32)
+        for g in range(len(groups)):
+            corner = corner + crossed(k, g, 1)
+        for kk in range(first):
+            piece = corner[:, kk * width : (kk + 1) * width]
+            ref["o_one"][k, tiles + kk] = ref["d_one"][k, kk] + piece
+        write(ref["o_one"].at[k, tiles:], ref["out_one"].at[k, tiles:])
+    result = ref["d_two"][0, 0]
+    for g in range(len(groups)):
+        result = result + crossed(chunks, g, 2)
     for step in range(1, cols):
         other = (c + step) % cols
         remote(
-            ref["b"].at[other], ref["b"].at[other], ref["b_send"].at[step], ref["b_recv"].at[other], r, other
+            ref["b"].at[other], ref["b"].at[other], ref["b_send"], ref["b_recv"].at[other], r, other
         ).wait_recv()
-    result = ref["d_two"][0, 0] + final[height:]
     for q in range(cols):
-        result = result - three(halves_of(ref["b"][q]), (ref["cl_h"][q], ref["cl_l"][q]))
+        span = slice(q * fringe, (q + 1) * fringe)
+        result = result - three(halves_of(ref["b"][q]), (ref["cl_h"][span], ref["cl_l"][span]))
     ref["o_two"][0, tiles + first] = result
     write(ref["o_two"].at[0, tiles:], ref["out_two"].at[0, tiles:])
 
-    for copy in sent:
-        copy.wait_send()
-    for go, copy in drains:
-
-        @pl.when(go)
-        def _(copy=copy):
-            copy().wait_send()
-
+    for go, wait in ends:
+        if go is None:
+            wait()
+        else:
+            pl.when(go)(wait)
     for copy in writes:
         copy.wait()
+
+
+def leave(one, two, out_one, out_two, held_one, held_two, sems):
+    pieces = [(one, held_one, out_one, k) for k in range(one.shape[0])] + [(two, held_two, out_two, 0)]
+
+    def copy(source, target, k, index):
+        return pltpu.make_async_copy(source.at[k], target.at[k], sems.at[index])
+
+    ins = [copy(a, b, k, n) for n, (a, b, _, k) in enumerate(pieces)]
+    outs = [copy(b, a, k, n + len(pieces)) for n, (_, b, a, k) in enumerate(pieces)]
+    for each in ins:
+        each.start()
+    for taken, given in zip(ins, outs):
+        taken.wait()
+        given.start()
+    for each in outs:
+        each.wait()
 
 
 def on_device_fused(
@@ -817,11 +880,14 @@
     low_slots = first * height // GRAIN * CAP
     col_slots = wide // GRAIN * CAP
     row_pad = -(-row_slots // 128) * 128
-    col_pad = -(-col_slots // 128) * 128
     edge = first * height
     fringe = first * width
     parts = min(3, tiles)
-    groups = [(i * tiles // parts, (i + 1) * tiles // parts) for i in range(parts)]
+    counts = [tiles // parts + (i < tiles % parts) for i in range(parts)]
+    if counts[-1] > 1:
+        counts[0] += 1
+        counts[-1] -= 1
+    groups = [(sum(counts[:i]), sum(counts[: i + 1])) for i in range(parts)]
     widest = max(stop - start for start, stop in groups) * width
     stages = chunks * parts
     dma = pltpu.SemaphoreType.DMA
@@ -829,8 +895,11 @@
         "a": pltpu.VMEM((tiles, tiles, height, width), F32),
         "d_one": pltpu.VMEM((first, first, height, width), F32),
         "d_two": pltpu.VMEM((1, 1, height, width), F32),
+        "l_one": pltpu.VMEM((entries,), jnp.int32),
+        "l_two": pltpu.VMEM((entries,), jnp.int32),
         "o_one": pltpu.VMEM((first, tiles + first, height, width), F32),
         "o_two": pltpu.VMEM((1, tiles + first + 1, height, width), F32),
+        "own": pltpu.VMEM((chunks, entries // rows, width), F32),
         "pall": pltpu.VMEM((chunks, entries, width), F32),
         "ph": pltpu.VMEM((entries, chunks * width), BF16),
         "pl": pltpu.VMEM((entries, chunks * width), BF16),
@@ -845,49 +914,51 @@
         "d_h": pltpu.VMEM((edge, fringe), BF16),
         "d_l": pltpu.VMEM((edge, fringe), BF16),
         "pick": pltpu.VMEM((2, col_slots, widest), BF16),
-        "s": pltpu.VMEM((2, cols, col_slots, 2 * height), F32),
-        "c1_h": pltpu.VMEM((cols, col_pad, fringe), BF16),
-        "c1_l": pltpu.VMEM((cols, col_pad, fringe), BF16),
-        "c2_h": pltpu.VMEM((cols, col_pad, width), BF16),
-        "c2_l": pltpu.VMEM((cols, col_pad, width), BF16),
-        "cl_h": pltpu.VMEM((cols, fringe, width), BF16),
-        "cl_l": pltpu.VMEM((cols, fringe, width), BF16),
+        "cl_h": pltpu.VMEM((cols * fringe, width), BF16),
+        "cl_l": pltpu.VMEM((cols * fringe, width), BF16),
         "b": pltpu.VMEM((cols, height, fringe), F32),
-        "l_sem": dma((3,)),
+        "l_sem": dma((5 + chunks,)),
         "w_sem": dma((stages + first + 1,)),
-        "g_send": dma((chunks, 7)),
-        "g_recv": dma((chunks, 7)),
-        "v_send": dma((chunks, 6)),
+        "g_send": dma((chunks,)),
+        "g_recv": dma((chunks, 4)),
+        "v_send": dma((chunks,)),
         "v_recv": dma((chunks, cols)),
-        "r_send": dma((stages, 7)),
-        "r_recv": dma((stages, 7)),
-        "s_send": dma((2, parts, 6)),
-        "s_recv": dma((2, parts, cols)),
-        "b_send": dma((cols,)),
+        "r_send": dma((stages,)),
+        "r_recv": dma((stages, 4)),
+        "s_send": dma((chunks + 1, parts)),
+        "s_recv": dma((chunks + 1, parts, cols)),
+        "b_send": dma,
         "b_recv": dma((cols,)),
     }
-    for s in range(stages):
-        k, g = (first, s - first * parts) if s >= first * parts else (s % first, s // first)
+    for g, (start, stop) in enumerate(groups):
+        count = (stop - start) * width // GRAIN * CAP // 2
+        region = -(-count * cols // 128) * 128
+        for n in range(chunks + 1):
+            scratch[f"s{n}{g}"] = pltpu.VMEM((cols, count, 2 * height), F32)
+        for name in ("h", "l"):
+            scratch[f"c1{g}{name}"] = pltpu.VMEM((2 * region, fringe), BF16)
+            scratch[f"c2{g}{name}"] = pltpu.VMEM((2 * region, width), BF16)
+    for s, (k, g) in enumerate(order_of(first, parts)):
         size = (groups[g][1] - groups[g][0]) * width
         if s == stages - 1:
             size += fringe
-        scratch[f"z{s}"] = pltpu.VMEM((2, 4, height, size), F32)
+        scratch[f"z{s}"] = pltpu.VMEM((8, height, size), F32)
         scratch[f"m{s}"] = pltpu.VMEM((4, height, size), F32)
         scratch[f"t{s}"] = pltpu.VMEM((4, height, size), F32)
         scratch[f"i{s}"] = pltpu.VMEM((2, height // 2, size), F32)
         scratch[f"f{s}"] = pltpu.VMEM((4, height // 2, size), F32)
     inputs = ["ancestor", "diag_one", "diag_two", "panel_one", "panel_two", "list_one", "list_two"]
     names = inputs + ["out_one", "out_two"] + list(scratch)
-    vmem = pl.BlockSpec(memory_space=pltpu.VMEM)
     hbm = pl.BlockSpec(memory_space=pl.ANY)
     dims = (rows, cols, height, width, tiles, first, entries, groups)
-    return pl.pallas_call(
+    shapes = (
+        jax.ShapeDtypeStruct((first, tiles + first, height, width), F32),
+        jax.ShapeDtypeStruct((1, tiles + first + 1, height, width), F32),
+    )
+    results = pl.pallas_call(
         functools.partial(fused, dims, names),
-        out_shape=(
-            jax.ShapeDtypeStruct((first, tiles + first, height, width), F32),
-            jax.ShapeDtypeStruct((1, tiles + first + 1, height, width), F32),
-        ),
-        in_specs=[hbm] * 3 + [vmem] * 4,
+        out_shape=shapes,
+        in_specs=[hbm] * len(inputs),
         out_specs=(hbm, hbm),
         scratch_shapes=list(scratch.values()),
         compiler_params=pltpu.CompilerParams(
@@ -897,11 +968,23 @@
         open_packed(ancestor, height, width),
         open_packed(inverse_first, height, width),
         open_packed(inverse_second, height, width),
-        panel_first.transpose(1, 0, 2),
-        panel_second.transpose(1, 0, 2),
+        panel_first,
+        panel_second,
         structure_first,
         structure_second,
     )
+    return pl.pallas_call(
+        leave,
+        out_shape=shapes,
+        in_specs=[hbm, hbm],
+        out_specs=(hbm, hbm),
+        scratch_shapes=[
+            pltpu.VMEM(shapes[0].shape, F32),
+            pltpu.VMEM(shapes[1].shape, F32),
+            dma((2 * (first + 1),)),
+        ],
+        compiler_params=pltpu.CompilerParams(vmem_limit_bytes=60 * 1024 * 1024),
+    )(*results)
 
 
 def fits(rows, cols):

time: 127 us -> 93.3 us (0.73)
  Pallas kernels: 121 us -> 92.3 us
  local copies, waits for them, and re-layouts: 5.43 us -> 0 us
    pallas_call x1 -> x2, Pallas kernels: 121 us -> 92.3 us  [the longest x1 90.3 us: on_device_fused(): pl.pallas_call(functools.partial(fused, dims, names), out_shape=shapes, i...]
    unnamed x3 -> x0, local copies, waits for them, and re-layouts: 5.43 us -> none
where the time goes in v3:
time: 93.3 us; the launch traced here: 93.1 us
  Pallas kernels  92.3 us (99%)
    pallas_call x1, Pallas kernels, on_device_fused(): pl.pallas_call(functools.partial(fused, dims, names), out_shape=shapes, i...  90.3 us
    pallas_call x1, Pallas kernels, on_device_fused(): pl.pallas_call(leave, out_shape=shapes, in_specs=[hbm, hbm], out_specs=(h...  2.02 us

profile of v3, /device:TPU:0, one launch (start us, length us, event | category | flops | bytes accessed | tf_op | source)
XLA Modules:
  0.0 93.1 jit_solution(9842405996530004377)
XLA Ops:
  0.6 90.3 %shard_map.86 = (f32[2,11,64,128]{3,2,1,0:T(8,128)}, f32[1,12,64,128]{3,2,1,0:T(8,128)}) custom-call(f32[9,9,64,128]{3,2,1,0:T(8,128)} %refs_0_.1, f32[2,2,64,128]{3,2,1,0:T(8,128)} %refs_1_.1, f32[1,1,64,128]{3,2,1,0:T(8,128)} %refs_2_.1, f32[192,2,128]{2,1,0:T(2,128)} %refs_3_.1, f32[192,1,128]{2,1,0:T(1,128)} %refs_4_.1, s32[1536]{0:T(1024)} %refs_5_.1, ...), custom_call_target="tpu_custom_call" | custom-call | tf_op jit(solution)/shard_map/pallas_call | solution.py:958
  91.0 2.0 %shard_map.87 = (f32[2,11,64,128]{3,2,1,0:T(8,128)}, f32[1,12,64,128]{3,2,1,0:T(8,128)}) custom-call(f32[2,11,64,128]{3,2,1,0:T(8,128)} %get-tuple-element.4.one, f32[1,12,64,128]{3,2,1,0:T(8,128)} %get-tuple-element.5.two), custom_call_target="tpu_custom_call" | custom-call | tf_op jit(solution)/shard_map/pallas_call | solution.py:976

commit v4 on v3

--- a/solution.py
+++ b/solution.py
@@ -293,7 +293,7 @@
     by_y = r + 4 - 8 * chip_y
     by_both = r + 6 - 4 * chip_x - 8 * chip_y
     mate = r + 1 - 2 * core
-    peers = {3: by_both, 1: by_x, 2: by_y}
+    peers = {1: by_x, 2: by_y, 3: by_both}
 
     def chip_at(rel):
         x = 1 - chip_x if rel % 2 else chip_x
@@ -484,11 +484,10 @@
             ref["v_one"][k, pl.ds(c, 1)] = picked[None, :row_slots]
         else:
             ref["v_two"][pl.ds(c, 1)] = picked[None, : row_slots + low_slots]
-        spread(*v_at(k))
         if k:
             forward(*v_at(k - 1))
-
-    keep(1, upper2, r_place2)
+        spread(*v_at(k))
+
     low_spot = spots(iota((128, entries), 0) == lower2, r_place2 - float(tall))
     spread_low = ones_at(low_spot == iota((128, edge), 1).astype(F32))
     loads["d_one"].wait()
@@ -509,9 +508,6 @@
             count = (stop - start) * width
             here = iota(((stop - start) * tile_slots, count), 1) + start * width
             ref["pick"][which, span, :count] = ones_at(spot[span] == here.astype(F32))
-
-    picker(0, c_owner1, c_slot1, c_place1)
-    picker(1, c_owner2, c_slot2, c_place2, above)
 
     def ready(k):
         arrive(*v_at(k))
@@ -610,7 +606,12 @@
         pass_on(s, 4, total.at[2, upper], ref[f"f{s}"].at[1], by_y)
         pair(0)
 
+    summed = set()
+
     def middle(s):
+        if s in summed:
+            return
+        summed.add(s)
         total = ref[f"t{s}"]
         live[s, 2].wait_recv()
 
@@ -721,20 +722,24 @@
         ref["cl_h"][...] = dd(take, ref["ph"][:, fringe:]).astype(BF16)
         ref["cl_l"][...] = dd(take, ref["pl"][:, fringe:]).astype(BF16)
 
-    asides = {0: [lambda: forward(*v_at(first))]}
-    for index, work in enumerate(
-        [lambda g=g: order_one(g) for g in range(len(groups))]
-        + [lambda g=g: order_two(g) for g in range(len(groups))]
-        + [order_low]
-    ):
-        asides.setdefault(1 + index // 2, []).append(work)
+    asides = {
+        1: [lambda: keep(1, upper2, r_place2)],
+        2: [
+            lambda: forward(*v_at(first)),
+            lambda: picker(0, c_owner1, c_slot1, c_place1),
+            lambda: picker(1, c_owner2, c_slot2, c_place2, above),
+        ],
+    }
+    for index, g in enumerate(range(len(groups))):
+        asides.setdefault(3 + index, []).append(lambda g=g: order_one(g))
     pending = []
     begun = set()
 
     def settle(s, now):
         if s not in done:
             finish(s)
-            pending.append((now + 2, stages[s]))
+            if stages[s][0] < first:
+                pending.append((now + 2, stages[s]))
 
     def relay(now):
         while pending and pending[0][0] <= now:
@@ -750,6 +755,8 @@
             begun.add(k)
             ready(k)
         if k >= first:
+            for s in range(first * len(groups)):
+                middle(s)
             for other in range(first):
                 settle(names_of[other, g], step)
         begin(step)
@@ -759,24 +766,24 @@
             middle(step - 2)
         push(step)
         relay(step)
-    for works in asides.values():
-        for work in works:
-            work()
     middle(count - 2)
-    relay(count)
-
-    def own_rows_of(g):
+    late = len(groups) - 1
+    for g in range(len(groups)):
+        if g == 1:
+            middle(count - 1)
+            relay(count + 2)
+        finish(stages.index((first, g)))
+        if g:
+            forward(*s_at(first, g - 1))
+    for g in range(len(groups)):
         choose(chunks, g)
-        pending.append((count + 2, (chunks, g)))
-
-    for index in range(len(groups)):
-        settle(count - len(groups) + index, count)
-        own_rows_of(index)
-        if index == 0:
-            middle(count - 1)
-        else:
-            relay(count + 2)
-    relay(count + 2)
+    for g in range(late):
+        order_two(g)
+    forward(*s_at(chunks, 0))
+    order_two(late)
+    order_low()
+    for g in range(1, late):
+        forward(*s_at(chunks, g))
 
     def side_by_side(n, g):
         region = counted(g)[1]
@@ -794,38 +801,37 @@
         near = three(both, ordered(at, g, 0))[:height]
         return near + three(both, ordered(at, g, 1))[height:]
 
-    cross = jnp.zeros((height, fringe), F32)
+    def corner(k):
+        total = jnp.zeros((height, fringe), F32)
+        for g in range(len(groups)):
+            total = total + crossed(k, g, 1)
+        for kk in range(first):
+            piece = total[:, kk * width : (kk + 1) * width]
+            ref["o_one"][k, tiles + kk] = ref["d_one"][k, kk] + piece
+        write(ref["o_one"].at[k, tiles:], ref["out_one"].at[k, tiles:])
+
+    tail = ref[f"t{len(stages) - 1}"]
+    cross = -tail[0, :, tail.shape[2] - fringe :]
     for g in range(len(groups)):
         cross = cross + crossed(first, g, 1)
-    tail = ref[f"t{len(stages) - 1}"]
-    bottom = cross - tail[0, :, tail.shape[2] - fringe :]
-    ref["b"][pl.ds(c, 1)] = bottom[None]
-    for step in range(1, cols):
-        other = (c + step) % cols
-        launch(
-            remote(
-                ref["b"].at[c], ref["b"].at[c], ref["b_send"], ref["b_recv"].at[c], r, other
-            )
-        )
-    sent(lambda: ref["b"].at[pl.ds(0, cols - 1)], ref["b_send"])
+    ref["b"][pl.ds(c, 1)] = cross[None]
+    b_at = (
+        ref["b"].at.__getitem__,
+        ref["b_send"],
+        ref["b_recv"],
+        lambda n: ref["b"].at[pl.ds(0, n)],
+    )
+    spread(*b_at)
     for kk in range(first):
-        ref["o_two"][0, tiles + kk] = bottom[:, kk * width : (kk + 1) * width]
-    for k in range(first):
-        corner = jnp.zeros((height, fringe), F32)
-        for g in range(len(groups)):
-            corner = corner + crossed(k, g, 1)
-        for kk in range(first):
-            piece = corner[:, kk * width : (kk + 1) * width]
-            ref["o_one"][k, tiles + kk] = ref["d_one"][k, kk] + piece
-        write(ref["o_one"].at[k, tiles:], ref["out_one"].at[k, tiles:])
+        ref["o_two"][0, tiles + kk] = cross[:, kk * width : (kk + 1) * width]
+    corner(0)
+    forward(*b_at)
+    for k in range(1, first):
+        corner(k)
     result = ref["d_two"][0, 0]
     for g in range(len(groups)):
         result = result + crossed(chunks, g, 2)
-    for step in range(1, cols):
-        other = (c + step) % cols
-        remote(
-            ref["b"].at[other], ref["b"].at[other], ref["b_send"], ref["b_recv"].at[other], r, other
-        ).wait_recv()
+    arrive(*b_at)
     for q in range(cols):
         span = slice(q * fringe, (q + 1) * fringe)
         result = result - three(halves_of(ref["b"][q]), (ref["cl_h"][span], ref["cl_l"][span]))

time: 93.3 us -> 87.9 us (0.942)
  Pallas kernels: 92.3 us -> 86.9 us
    pallas_call x1, Pallas kernels: 90.3 us -> 84.8 us  [on_device_fused(): pl.pallas_call(functools.partial(fused, dims, names), out_shape=shapes, i...]
where the time goes in v4:
time: 87.9 us; the launch traced here: 87.7 us
  Pallas kernels  86.9 us (99%)
    pallas_call x1, Pallas kernels, on_device_fused(): pl.pallas_call(functools.partial(fused, dims, names), out_shape=shapes, i...  84.8 us
    pallas_call x1, Pallas kernels, on_device_fused(): pl.pallas_call(leave, out_shape=shapes, in_specs=[hbm, hbm], out_specs=(h...  2.02 us

profile of v4, /device:TPU:0, one launch (start us, length us, event | category | flops | bytes accessed | tf_op | source)
XLA Modules:
  0.0 87.7 jit_solution(17439793883367030472)
XLA Ops:
  0.6 84.8 %shard_map.86 = (f32[2,11,64,128]{3,2,1,0:T(8,128)}, f32[1,12,64,128]{3,2,1,0:T(8,128)}) custom-call(f32[9,9,64,128]{3,2,1,0:T(8,128)} %refs_0_.1, f32[2,2,64,128]{3,2,1,0:T(8,128)} %refs_1_.1, f32[1,1,64,128]{3,2,1,0:T(8,128)} %refs_2_.1, f32[192,2,128]{2,1,0:T(2,128)} %refs_3_.1, f32[192,1,128]{2,1,0:T(1,128)} %refs_4_.1, s32[1536]{0:T(1024)} %refs_5_.1, ...), custom_call_target="tpu_custom_call" | custom-call | tf_op jit(solution)/shard_map/pallas_call | solution.py:964
  85.5 2.0 %shard_map.87 = (f32[2,11,64,128]{3,2,1,0:T(8,128)}, f32[1,12,64,128]{3,2,1,0:T(8,128)}) custom-call(f32[2,11,64,128]{3,2,1,0:T(8,128)} %get-tuple-element.4.one, f32[1,12,64,128]{3,2,1,0:T(8,128)} %get-tuple-element.5.two), custom_call_target="tpu_custom_call" | custom-call | tf_op jit(solution)/shard_map/pallas_call | solution.py:982

commit v5 on v4

--- a/solution.py
+++ b/solution.py
@@ -760,10 +760,10 @@
             for other in range(first):
                 settle(names_of[other, g], step)
         begin(step)
+        if step >= 2:
+            middle(step - 2)
         for work in asides.pop(step, []):
             work()
-        if step >= 2:
-            middle(step - 2)
         push(step)
         relay(step)
     middle(count - 2)

time: 87.9 us -> 86.5 us (0.984)
  Pallas kernels: 86.9 us -> 85.6 us
    pallas_call x1, Pallas kernels: 84.8 us -> 83.5 us  [on_device_fused(): pl.pallas_call(functools.partial(fused, dims, names), out_shape=shapes, i...]
where the time goes in v5:
time: 86.5 us; the launch traced here: 86.4 us
  Pallas kernels  85.6 us (99%)
    pallas_call x1, Pallas kernels, on_device_fused(): pl.pallas_call(functools.partial(fused, dims, names), out_shape=shapes, i...  83.5 us
    pallas_call x1, Pallas kernels, on_device_fused(): pl.pallas_call(leave, out_shape=shapes, in_specs=[hbm, hbm], out_specs=(h...  2.02 us

profile of v5, /device:TPU:0, one launch (start us, length us, event | category | flops | bytes accessed | tf_op | source)
XLA Modules:
  0.0 86.4 jit_solution(9018039403541527043)
XLA Ops:
  0.6 83.5 %shard_map.86 = (f32[2,11,64,128]{3,2,1,0:T(8,128)}, f32[1,12,64,128]{3,2,1,0:T(8,128)}) custom-call(f32[9,9,64,128]{3,2,1,0:T(8,128)} %refs_0_.1, f32[2,2,64,128]{3,2,1,0:T(8,128)} %refs_1_.1, f32[1,1,64,128]{3,2,1,0:T(8,128)} %refs_2_.1, f32[192,2,128]{2,1,0:T(2,128)} %refs_3_.1, f32[192,1,128]{2,1,0:T(1,128)} %refs_4_.1, s32[1536]{0:T(1024)} %refs_5_.1, ...), custom_call_target="tpu_custom_call" | custom-call | tf_op jit(solution)/shard_map/pallas_call | solution.py:964
  84.2 2.0 %shard_map.87 = (f32[2,11,64,128]{3,2,1,0:T(8,128)}, f32[1,12,64,128]{3,2,1,0:T(8,128)}) custom-call(f32[2,11,64,128]{3,2,1,0:T(8,128)} %get-tuple-element.4.one, f32[1,12,64,128]{3,2,1,0:T(8,128)} %get-tuple-element.5.two), custom_call_target="tpu_custom_call" | custom-call | tf_op jit(solution)/shard_map/pallas_call | solution.py:982
